TPU v7x, 256 devices: a whole 4x4x8 slice. The times are simulated.
256 devices in a mesh: gx: 32 (over z, y_hi, core), gy: 8 (over y_lo, x).
Axes of the slice: x: 4, y: 4 (y_hi: 2, y_lo: 2; y = y_hi * 2 + y_lo), z: 8, core: 2. Of those that a mesh axis runs over, the one named last changes fastest.
Arguments:
- prognostic_values: float32 [3, 6, 4096, 4096], P(None, None, 'gx', 'gy'), may hold values from -6 to 6
- forcing_host_values: bfloat16 [3, 6, 4096, 4096], P(None, None, 'gx', 'gy'), may hold values from -6 to 6
- strength: float32 [3, 6], replicated, may hold values from 50 to 200
- level_height: float32 [3], replicated, may hold values from 0.2 to 3
- pbl_height: float32 [4096, 4096], P('gx', 'gy'), may hold values from 0.2 to 3
Outputs:
- tendency: bfloat16 [3, 6, 4096, 4096], P(None, None, 'gx', 'gy')
- energy: float32 [3, 6], replicated
All inputs are finite; a program needn't handle non-finite values.
Results may differ from a plain program's by a relative error of at most 0.001.
Values sent between devices are 32-bit elements; how exact they have to be, the bound alone decides.
No kernel may reach another device: no remote copies, remote signals or barrier semaphores. Data moves between devices by JAX's collectives and lax.ppermute only.
A program may use at most 64 MiB of HBM per device.

v0:
```python
import jax
import jax.numpy as jnp
from jax import lax
from jax.sharding import PartitionSpec as P

KX = 32
KY = 32


ramp_depth = 0.25


def from_everyone(value, axis):
    copies = jnp.broadcast_to(value, (lax.axis_size(axis), *value.shape))
    return lax.all_to_all(copies, axis, split_axis=0, concat_axis=0, tiled=True)


def taken_together(value, axis):
    everything = from_everyone(value, axis)
    return jnp.sum(everything, axis=0)


def padded_to(lines, devices):
    spare = -lines.shape[0] % devices
    if not spare:
        return lines
    return jnp.concatenate([lines, jnp.zeros((spare, *lines.shape[1:]), lines.dtype)])


def laid_out(blocks, dim):
    lengths = list(blocks.shape[1:])
    lengths[dim] *= blocks.shape[0]
    return jnp.moveaxis(blocks, 0, dim).reshape(lengths)


def gather_directly(value, axis, dim):
    return laid_out(from_everyone(value, axis), dim)


def in_blocks(value, dim, devices):
    lengths = value.shape
    blocks = value.reshape(*lengths[:dim], devices, lengths[dim] // devices, *lengths[dim + 1 :])
    return jnp.moveaxis(blocks, dim, 0)


def summed_on_arrival(value, axis, dim):
    devices = lax.axis_size(axis)
    blocks = lax.all_to_all(in_blocks(value, dim, devices), axis, 0, 0, tiled=True)
    return jnp.sum(blocks, axis=0)


def sum_by_parts(value, axes):
    lines = value.reshape(-1, value.shape[-1])
    padded = padded_to(lines, lax.axis_size(axes))
    whole = gather_directly(summed_on_arrival(padded, axes, 0), axes, 0)
    return lax.slice_in_dim(whole, 0, len(lines)).reshape(value.shape)


def cosine_table(total, modes, start, count):
    index = (start + jnp.arange(count)).astype(jnp.float32)
    waves = jnp.arange(modes).astype(jnp.float32)
    scales = jnp.where(waves == 0.0, jnp.sqrt(1.0 / total), jnp.sqrt(2.0 / total)).astype(
        jnp.float32
    )
    return scales[None, :] * jnp.cos(jnp.pi * (index[:, None] + 0.5) * waves[None, :] / total)


def per_device(prognostic_values, forcing_host_values, strength, level_height, pbl_height):
    rows = prognostic_values.shape[2]
    cols = prognostic_values.shape[3]
    largest_wavenumber = lax.Precision.HIGHEST
    row_table = cosine_table(rows * lax.axis_size("gx"), KX, lax.axis_index("gx") * rows, rows)
    col_table = cosine_table(cols * lax.axis_size("gy"), KY, lax.axis_index("gy") * cols, cols)
    diff = forcing_host_values.astype(jnp.float32) - prognostic_values
    part = jnp.einsum("...ij,jb->...ib", diff, col_table, precision=largest_wavenumber)
    within = taken_together(
        jnp.einsum("ia,...ib->...ab", row_table, part, precision=largest_wavenumber), "gy"
    )
    mode_factors = sum_by_parts(within, "gx")
    restored_fields = jnp.einsum(
        "ia,lvab->lvib", row_table, mode_factors, precision=largest_wavenumber
    )
    recon = jnp.einsum("lvib,jb->lvij", restored_fields, col_table, precision=largest_wavenumber)
    damping_share = 1.0 / (
        1.0 + jnp.exp(-(level_height[:, None, None] - pbl_height[None]) / ramp_depth)
    )
    tendency = (strength[:, :, None, None] * damping_share[:, None] * recon).astype(jnp.bfloat16)
    energy = jnp.sum(mode_factors * mode_factors, axis=(2, 3)) / (KX * KY)
    return (tendency, energy)


def solution(mesh):
    return jax.shard_map(
        per_device,
        mesh=mesh,
        in_specs=(P(None, None, "gx", "gy"), P(None, None, "gx", "gy"), P(), P(), P("gx", "gy")),
        out_specs=(P(None, None, "gx", "gy"), P()),
        check_vma=False,
    )
```

profile of v0, /device:TPU:1, one launch (start us, length us, event | category | flops | bytes accessed | tf_op | source)
XLA Modules:
  0.0 76.3 jit_solution(3102247311464418814)
XLA Ops:
  0.7 7.3 %fusion = f32[3,6,128,32]{2,3,1,0:T(8,128)S(1)} fusion(f32[3,6,128,512]{3,2,1,0:T(8,128)} %param.5, bf16[3,6,128,512]{3,2,1,0:T(8,128)(2,1)} %param.6, f32[32]{0:T(128)S(1)} %iota_convert_fusion, f32[512]{0:T(512)S(1)} %add_multiply_fusion, f32[32]{0:T(128)S(1)} %compare_select_fusion), kind=kOutput, calls=%fused_computation.1 | convolution fusion | flops 455393280 | bytes 7375104 | tf_op jit(solution)/shard_map/...ij,jb->...ib/dot_general | solution.py:75
  8.0 0.5 convolution_bitcast_fusion.1
  8.5 0.1 copy.9
  8.6 0.3 broadcast_in_dim.28
  8.9 1.0 %reshape.42 = f32[8,1,18432]{2,1,0:T(1,128)S(1)} reshape(f32[8,3,6,32,32]{4,3,2,1,0:T(8,128)S(1)} %broadcast_in_dim.28) | data formatting | bytes 1179648
  10.0 15.3 %all_to_all.15 = f32[8,1,18432]{2,1,0:T(1,128)S(1)} all-to-all(f32[8,1,18432]{2,1,0:T(1,128)S(1)} %reshape.42), channel_id=1, replica_groups=mesh['gx'=32,'gy'=8] {'gy'}, dimensions={0} | all-to-all | bytes 1179648 | tf_op jit(solution)/shard_map/all_to_all | solution.py:15
  25.3 0.5 broadcast.82
  25.8 2.0 %reduce.2 = f32[8,18432]{1,0:T(8,128)S(1)} reduce(f32[8,1,18432]{2,1,0:T(1,128)S(1)} %all_to_all.15, f32[]{:T(128)} %broadcast.82), dimensions={1}, to_apply=%all_to_all.9.reduce_sub_computation | reduce | bytes 1179652 | tf_op jit(solution)/shard_map/all_to_all | solution.py:15
  27.9 0.8 %reshape.43 = f32[8,3,6,32,32]{4,3,2,1,0:T(8,128)S(1)} reshape(f32[8,18432]{1,0:T(8,128)S(1)} %reduce.2) | data formatting | bytes 1179648
  28.7 0.3 reduce_sum.34
  29.0 0.2 reshape.44
  29.2 22.9 %all_to_all.16 = f32[32,1,576]{2,1,0:T(1,128)S(1)} all-to-all(f32[32,1,576]{2,1,0:T(1,128)S(1)} %reshape.44), channel_id=1, replica_groups=mesh['gx'=32,'gy'=8] {'gx'}, dimensions={0} | all-to-all | bytes 147456 | tf_op jit(solution)/shard_map/all_to_all | solution.py:48
  52.1 0.8 %reduce.3 = f32[32,576]{1,0:T(8,128)S(1)} reduce(f32[32,1,576]{2,1,0:T(1,128)S(1)} %all_to_all.16, f32[]{:T(128)} %broadcast.82), dimensions={1}, to_apply=%all_to_all.10.reduce_sub_computation | reduce | bytes 147460 | tf_op jit(solution)/shard_map/all_to_all | solution.py:48
  53.0 0.1 reshape.45
  53.2 0.8 %reshape.46 = f32[32,1,576]{2,1,0:T(1,128)} reshape(f32[32,18,32]{2,1,0:T(8,128)S(1)} %broadcast_in_dim.29) | data formatting | bytes 147456
  54.0 3.8 %all-to-all-start.2 = ((f32[32,1,576]{2,1,0:T(1,128)}), f32[32,1,576]{2,1,0:T(1,128)S(1)}, u32[]{:S(2)}, u32[]{:S(2)}) async-start(f32[32,1,576]{2,1,0:T(1,128)} %reshape.46), calls=%async_computation.2 | async-start | bytes 163840 | tf_op jit(solution)/shard_map/all_to_all | solution.py:15
  57.9 0.3 add_divide_fusion
  58.2 9.8 %all-to-all-done.2 = f32[32,1,576]{2,1,0:T(1,128)S(1)} async-done(((f32[32,1,576]{2,1,0:T(1,128)}), f32[32,1,576]{2,1,0:T(1,128)S(1)}, u32[]{:S(2)}, u32[]{:S(2)}) %all-to-all-start.2) | async-done | bytes 73760 | tf_op jit(solution)/shard_map/all_to_all | solution.py:15
  67.9 0.8 %reduce.4 = f32[32,576]{1,0:T(8,128)S(1)} reduce(f32[32,1,576]{2,1,0:T(1,128)S(1)} %all-to-all-done.2, f32[]{:T(128)} %broadcast.82), dimensions={1}, to_apply=%all_to_all.11.reduce_sub_computation | reduce | bytes 147460 | tf_op jit(solution)/shard_map/all_to_all | solution.py:15
  68.8 0.1 reshape.47
  68.9 0.2 multiply_reduce_fusion
  69.3 0.7 convolution_bitcast_fusion
  70.0 0.6 broadcast_multiply_fusion
  70.6 5.7 %multiply_convert_fusion = bf16[3,6,128,512]{3,2,1,0:T(8,128)(2,1)} fusion(f32[3,128,512]{2,1,0:T(8,128)S(1)} %add_divide_fusion, f32[3,6]{1,0:T(4,128)S(1)} %copy-done.2, f32[3,6,128,32]{2,3,1,0:T(8,128)S(1)} %convolution_bitcast_fusion, f32[32]{0:T(128)S(1)} %iota_convert_fusion, f32[512]{0:T(512)S(1)} %add_multiply_fusion, f32[32]{0:T(128)S(1)} %compare_select_fusion), kind=kOutput, calls=%fused_computation | convolution fusion | flops 456572928 | bytes 3443016 | tf_op jit(solution)/shard_map/lvib,jb->lvij/dot_general | solution.py:83
  (16 shorter events, 0.3 us)
Async XLA Ops:
  27.9 30.0 %copy-start = (f32[128,512]{1,0:T(8,128)S(1)}, f32[128,512]{1,0:T(8,128)}, u32[]{:S(2)}) copy-start(f32[128,512]{1,0:T(8,128)} %param.9) | copy-start | bytes 786436
  27.9 30.0 %copy-start.1 = (f32[3]{0:T(128)S(1)}, f32[3]{0:T(128)}, u32[]{:S(2)}) copy-start(f32[3]{0:T(128)} %param.8) | copy-start | bytes 40
  28.7 41.9 %copy-start.2 = (f32[3,6]{1,0:T(4,128)S(1)}, f32[3,6]{1,0:T(4,128)}, u32[]{:S(2)}) copy-start(f32[3,6]{1,0:T(4,128)} %param.7) | copy-start | bytes 220
  54.0 13.9 %all-to-all-start.2 = ((f32[32,1,576]{2,1,0:T(1,128)}), f32[32,1,576]{2,1,0:T(1,128)S(1)}, u32[]{:S(2)}, u32[]{:S(2)}) async-start(f32[32,1,576]{2,1,0:T(1,128)} %reshape.46), calls=%async_computation.2 | async-start | bytes 163840 | tf_op jit(solution)/shard_map/all_to_all | solution.py:15
where the time goes:
time: 76.6 us; the launch traced here: 76.3 us
  blocking collectives  38.3 us (50%)
  matrix products  14.2 us (19%)
  waiting for transfers between devices  9.77 us (13%)
  other arithmetic  5.2 us (7%)
  local copies, waits for them, and re-layouts  4.16 us (5%)
  starting transfers between devices  3.85 us (5%)
  between operations  0.87 us (1%)
    all_to_all x1, blocking collectives, summed_on_arrival(): lax.all_to_all(in_blocks(value, dim, devices), axis, 0, 0, tiled=True)  22.9 us
    all_to_all x1, blocking collectives, from_everyone(): return lax.all_to_all(copies, axis, split_axis=0, concat_axis=0, tiled=True)  15.3 us
    all_to_all x1, waiting for transfers between devices, from_everyone(): return lax.all_to_all(copies, axis, split_axis=0, concat_axis=0, tiled=True)  9.77 us
    dot_general x1, matrix products, per_device(): jnp.einsum('...ij,jb->...ib', diff, col_table, precision=largest_wavenumber)  7.28 us
    dot_general x1, matrix products, per_device(): jnp.einsum('lvib,jb->lvij', restored_fields, col_table, precision=largest...  5.74 us
    all_to_all x1, starting transfers between devices, from_everyone(): return lax.all_to_all(copies, axis, split_axis=0, concat_axis=0, tiled=True)  3.85 us
    unnamed x12, local copies, waits for them, and re-layouts  3.05 us
    all_to_all x2, other arithmetic, from_everyone(): return lax.all_to_all(copies, axis, split_axis=0, concat_axis=0, tiled=True)  2.88 us
  transfers between devices with their start and end apart: 1, of which 1 were waited for; matrix products, arithmetic and copies ran while one was open for 0% of the time, Pallas kernels for 0%

commit v1 on v0

v1 whole, which is shorter than its diff:
```python
import math

import jax
import jax.numpy as jnp
from jax import lax
from jax.experimental import pallas as pl
from jax.experimental.pallas import tpu as pltpu
from jax.sharding import PartitionSpec as P

MODES = 32
RAMP = 0.25
BOTH = ("gx", "gy")
F32, BF16 = jnp.float32, jnp.bfloat16


def position(x, y, z, core):
    return ((z * 4 + (y // 2) * 2 + core) * 8) + (y % 2) * 4 + x


def grouped(key, order):
    found = {}
    for z in range(8):
        for y in range(4):
            for x in range(4):
                for core in range(2):
                    place = (x, y, z, core)
                    found.setdefault(key(*place), []).append((order(*place), position(*place)))
    return [[at for _, at in sorted(group)] for _, group in sorted(found.items())]


SHARE = (0, 1, 1, 0)
NEAR = grouped(lambda x, y, z, c: (y // 2, z), lambda x, y, z, c: (SHARE[y], x, c))
FAR = grouped(lambda x, y, z, c: (x, SHARE[y], c), lambda x, y, z, c: (z, y))
SHARES = 16


def cosines(index, wave, total):
    turn = ((2 * index + 1) * wave) & (4 * total - 1)
    turn = jnp.where(turn > 2 * total, 4 * total - turn, turn)
    y = (total - turn).astype(F32) * F32(math.pi / (2 * total))
    square = y * y
    series = F32(1.0 / math.factorial(13))
    for power in (11, 9, 7, 5, 3, 1):
        sign = -1.0 if power % 4 == 3 else 1.0
        series = series * square + F32(sign / math.factorial(power))
    scale = jnp.where(wave == 0, F32(math.sqrt(1.0 / total)), F32(math.sqrt(2.0 / total)))
    return scale * (y * series)


def split(value):
    high = value.astype(BF16)
    return high, (value - high.astype(F32)).astype(BF16)


def iota(shape, dim):
    return lax.broadcasted_iota(jnp.int32, shape, dim)


def dot(a, b):
    return jnp.dot(a, b, preferred_element_type=F32)


def analysis(levels, variables, nx, ny, p_hbm, f_hbm, out_ref, p_buf, f_buf, p_sem, f_sem, w_ref):
    rows, cols = p_hbm.shape[2], p_hbm.shape[3]
    fields = [(l, v) for l in range(levels) for v in range(variables)]
    copies = []
    for k, (l, v) in enumerate(fields):
        pair = (
            pltpu.make_async_copy(p_hbm.at[l, v], p_buf.at[k], p_sem.at[k]),
            pltpu.make_async_copy(f_hbm.at[l, v], f_buf.at[k], f_sem.at[k]),
        )
        for copy in pair:
            copy.start()
        copies.append(pair)

    row0 = lax.axis_index("gx") * rows
    col0 = lax.axis_index("gy") * cols
    wide = 4 * MODES
    table = cosines(col0 + iota((cols, wide), 0), iota((cols, wide), 1) & (MODES - 1), ny)
    high, low = split(table)
    w_ref[:, :wide] = high
    w_ref[:, wide:] = low
    table = cosines(row0 + iota((MODES, rows), 1), iota((MODES, rows), 0), nx)
    row_table = jnp.concatenate(split(table), axis=0)
    lane_group = iota((8, wide), 1) // MODES

    for k in range(len(fields)):
        for copy in copies[k]:
            copy.wait()
        diff_high, diff_low = split(f_buf[k].astype(F32) - p_buf[k])
        both = dot(diff_high, w_ref[...]) + dot(diff_low, w_ref[...])
        part_high, part_low = split(both[:, :wide] + both[:, wide:])
        both = dot(row_table, part_high) + dot(row_table, part_low)
        coefs = both[:MODES] + both[MODES:]
        tile = coefs[:8]
        for q in range(1, 4):
            tile = jnp.where(lane_group == q, coefs[8 * q : 8 * q + 8], tile)
        out_ref[8 * k : 8 * k + 8, :] = tile


def synthesis(
    levels, variables, nx, ny,
    strength_ref, level_ref, c_ref, pbl_ref, out_hbm, energy_ref, o_buf, weight_ref, o_sem, t_ref,
):
    rows, cols = pbl_ref.shape
    row0 = lax.axis_index("gx") * rows
    col0 = lax.axis_index("gy") * cols
    wide = 4 * MODES
    for l in range(levels):
        weight_ref[l] = 1.0 / (1.0 + jnp.exp(-(level_ref[l] - pbl_ref[...]) / F32(RAMP)))
    lane_group = iota((1, wide), 1) // MODES
    high, low = split(cosines(row0 + iota((rows, wide), 0), iota((rows, wide), 1) & (MODES - 1), nx))
    none = jnp.zeros_like(high)
    row_table = jnp.where(lane_group < 2, high, jnp.where(lane_group == 2, low, none))
    high, low = split(cosines(col0 + iota((MODES, cols), 1), iota((MODES, cols), 0), ny))
    t_ref[0:32, :] = high
    t_ref[32:64, :] = high
    t_ref[64:96, :] = low
    t_ref[96:128, :] = jnp.zeros_like(high)

    at = (iota((levels, variables), 0), iota((levels, variables), 1))
    energy = jnp.zeros((levels, variables), F32)
    copies = []
    for l in range(levels):
        for v in range(variables):
            k = l * variables + v
            tile = c_ref[8 * k : 8 * k + 8, :]
            total = jnp.sum(tile * tile) / F32(MODES * MODES)
            energy = jnp.where((at[0] == l) & (at[1] == v), total, energy)
            tile = tile * strength_ref[l, v]
            blocks = []
            for q in range(4):
                one = jnp.where(lane_group == q, tile, 0.0)
                one = one + pltpu.roll(one, MODES, 1)
                blocks.append(one + pltpu.roll(one, 2 * MODES, 1))
            high, low = split(jnp.concatenate(blocks, axis=0))
            coefs = jnp.concatenate([high, low, high, jnp.zeros_like(high)], axis=0)
            high, low = split(dot(row_table, coefs))
            restored = jnp.where(lane_group == 1, low, high)
            recon = dot(restored, t_ref[...])
            o_buf[k] = (weight_ref[l] * recon).astype(BF16)
            copy = pltpu.make_async_copy(o_buf.at[k], out_hbm.at[l, v], o_sem.at[k])
            copy.start()
            copies.append(copy)
    energy_ref[...] = energy
    for copy in copies:
        copy.wait()


def per_device(prognostic_values, forcing_host_values, strength, level_height, pbl_height):
    levels, variables, rows, cols = prognostic_values.shape
    nx, ny = rows * lax.axis_size("gx"), cols * lax.axis_size("gy")
    count = levels * variables
    lines = 8 * count
    shapes = (levels, variables, nx, ny)
    anywhere = pl.BlockSpec(memory_space=pl.ANY)
    vmem = pl.BlockSpec(memory_space=pltpu.VMEM)
    smem = pl.BlockSpec(memory_space=pltpu.SMEM)

    mine = pl.pallas_call(
        lambda *refs: analysis(*shapes, *refs),
        name="analysis",
        out_shape=jax.ShapeDtypeStruct((lines, 128), F32),
        in_specs=[anywhere, anywhere],
        out_specs=vmem,
        scratch_shapes=[
            pltpu.VMEM((count, rows, cols), F32),
            pltpu.VMEM((count, rows, cols), BF16),
            pltpu.SemaphoreType.DMA((count,)),
            pltpu.SemaphoreType.DMA((count,)),
            pltpu.VMEM((cols, 8 * MODES), BF16),
        ],
    )(prognostic_values, forcing_host_values)

    length = lines * 128 // SHARES
    shares = mine.reshape(SHARES, 1, length)
    got = lax.all_to_all(shares, BOTH, 0, 0, tiled=True, axis_index_groups=NEAR)
    share = jnp.broadcast_to(jnp.sum(got, axis=0, keepdims=True), (SHARES, 1, length))
    got = lax.all_to_all(share, BOTH, 0, 0, tiled=True, axis_index_groups=FAR)
    share = jnp.broadcast_to(jnp.sum(got, axis=0, keepdims=True), (SHARES, 1, length))
    coefs = lax.all_to_all(share, BOTH, 0, 0, tiled=True, axis_index_groups=NEAR)
    coefs = coefs.reshape(lines, 128)

    tendency, energy = pl.pallas_call(
        lambda *refs: synthesis(*shapes, *refs),
        name="synthesis",
        out_shape=(
            jax.ShapeDtypeStruct((levels, variables, rows, cols), BF16),
            jax.ShapeDtypeStruct((levels, variables), F32),
        ),
        in_specs=[smem, smem, vmem, vmem],
        out_specs=(anywhere, vmem),
        scratch_shapes=[
            pltpu.VMEM((count, rows, cols), BF16),
            pltpu.VMEM((levels, rows, cols), F32),
            pltpu.SemaphoreType.DMA((count,)),
            pltpu.VMEM((4 * MODES, cols), BF16),
        ],
    )(strength, level_height, coefs, pbl_height)
    return tendency, energy


def solution(mesh):
    return jax.shard_map(
        per_device,
        mesh=mesh,
        in_specs=(P(None, None, "gx", "gy"), P(None, None, "gx", "gy"), P(), P(), P("gx", "gy")),
        out_specs=(P(None, None, "gx", "gy"), P()),
        check_vma=False,
    )
```

time: 76.6 us -> 59 us (0.77)
  Pallas kernels: 0 us -> 15.5 us
  matrix products: 14.2 us -> 0 us
  waiting for transfers between devices: 9.77 us -> 0 us
  other arithmetic: 5.2 us -> 0.11 us
  local copies, waits for them, and re-layouts: 4.16 us -> 0.08 us
  blocking collectives: 38.3 us -> 42.3 us
  starting transfers between devices: 3.85 us -> 0 us
    pallas_call x0 -> x2, Pallas kernels: none -> 15.5 us  [the longest x1 9.73 us: per_device(): pl.pallas_call(lambda *refs: analysis(*shapes, *refs), name='analysis', o...]
    dot_general x4 -> x0, matrix products: 14.2 us -> none  [the longest x1 7.28 us: per_device(): jnp.einsum('...ij,jb->...ib', diff, col_table, precision=largest_wavenumber)]
    all_to_all x1 -> x0, waiting for transfers between devices: 9.77 us -> none  [from_everyone(): return lax.all_to_all(copies, axis, split_axis=0, concat_axis=0, tiled=True)]
    all_to_all x2 -> x3, blocking collectives: 38.3 us -> 42.3 us  [the longest x1 18.9 us: per_device(): got = lax.all_to_all(share, BOTH, 0, 0, tiled=True, axis_index_groups=FAR)]
    all_to_all x1 -> x0, starting transfers between devices: 3.85 us -> none  [from_everyone(): return lax.all_to_all(copies, axis, split_axis=0, concat_axis=0, tiled=True)]
    all_to_all x3 -> x0, other arithmetic: 3.71 us -> none  [the longest x2 2.88 us: from_everyone(): return lax.all_to_all(copies, axis, split_axis=0, concat_axis=0, tiled=True)]
    unnamed x12 -> x0, local copies, waits for them, and re-layouts: 3.05 us -> none
    div x2 -> x0, other arithmetic: 0.87 us -> none  [the longest x1 0.58 us: per_device(): energy = jnp.sum(mode_factors * mode_factors, axis=(2, 3)) / (KX * KY)]
  transfers between devices with their start and end apart: 1 -> 0, of which waited for: 1 -> 0; matrix products, arithmetic and copies ran while one was open for 0% -> 0% of each run, Pallas kernels for 0% -> 0%
where the time goes in v1:
time: 59 us; the launch traced here: 58.7 us
  blocking collectives  42.3 us (72%)
  Pallas kernels  15.5 us (26%)
  between operations  0.66 us (1%)
    all_to_all x1, blocking collectives, per_device(): got = lax.all_to_all(share, BOTH, 0, 0, tiled=True, axis_index_groups=FAR)  18.9 us
    all_to_all x1, blocking collectives, per_device(): got = lax.all_to_all(shares, BOTH, 0, 0, tiled=True, axis_index_groups=NEAR)  12.7 us
    all_to_all x1, blocking collectives, per_device(): lax.all_to_all(share, BOTH, 0, 0, tiled=True, axis_index_groups=NEAR)  10.8 us
    pallas_call x1, Pallas kernels, per_device(): pl.pallas_call(lambda *refs: analysis(*shapes, *refs), name='analysis', o...  9.73 us
    pallas_call x1, Pallas kernels, per_device(): pl.pallas_call(lambda *refs: synthesis(*shapes, *refs), name='synthesis',...  5.75 us

profile of v1, /device:TPU:1, one launch (start us, length us, event | category | flops | bytes accessed | tf_op | source)
XLA Modules:
  0.0 58.7 jit_solution(7410580683901181497)
XLA Ops:
  0.6 9.7 %analysis.1 = f32[144,128]{1,0:T(8,128)} custom-call(f32[3,6,128,512]{3,2,1,0:T(8,128)} %refs_0_.2, bf16[3,6,128,512]{3,2,1,0:T(8,128)(2,1)} %refs_1_.2), custom_call_target="tpu_custom_call" | custom-call | tf_op jit(solution)/shard_map/analysis/pallas_call | solution.py:160
  10.4 12.7 %all_to_all.15 = f32[16,1,1152]{2,1,0:T(1,128)S(1)} all-to-all(f32[16,1,1152]{2,1,0:T(1,128)} %bitcast.3), channel_id=1, replica_groups={{0,8,1,9,2,10,3,11,4,12,5,13,6,14,7,15},{32,40,33,41,34,42,35,43,36,44,..., dimensions={0} | all-to-all | bytes 147456 | tf_op jit(solution)/shard_map/all_to_all | solution.py:177
  23.0 0.1 reduce_sum.18
  23.1 18.9 %all_to_all.16 = f32[16,1,1152]{2,1,0:T(1,128)S(1)} all-to-all(f32[16,1,1152]{2,1,0:T(1,128)S(1)} %broadcast_in_dim.4), channel_id=1, replica_groups={{0,20,32,52,64,84,96,116,128,148,160,180,192,212,224,244},{8,28,40,60,7..., dimensions={0} | all-to-all | bytes 147456 | tf_op jit(solution)/shard_map/all_to_all | solution.py:179
  42.0 0.1 reduce_sum.19
  42.1 10.8 %all_to_all.17 = f32[16,1,1152]{2,1,0:T(1,128)} all-to-all(f32[16,1,1152]{2,1,0:T(1,128)S(1)} %broadcast_in_dim.5), channel_id=1, replica_groups={{0,8,1,9,2,10,3,11,4,12,5,13,6,14,7,15},{32,40,33,41,34,42,35,43,36,44,..., dimensions={0} | all-to-all | bytes 147456 | tf_op jit(solution)/shard_map/all_to_all | solution.py:181
  52.9 5.8 %synthesis.1 = (bf16[3,6,128,512]{3,2,1,0:T(8,128)(2,1)}, f32[3,6]{1,0:T(4,128)}) custom-call(f32[3,6]{1,0:T(4,128)} %refs_0_.3, f32[3]{0:T(128)} %refs_1_.3, f32[144,128]{1,0:T(8,128)} %bitcast.2, f32[128,512]{1,0:T(8,128)} %refs_3_.1), custom_call_target="tpu_custom_call" | custom-call | tf_op jit(solution)/shard_map/synthesis/pallas_call | solution.py:184
  (2 shorter events, 0.1 us)

commit v2 on v1

v2 whole, which is shorter than its diff:
```python
import math

import jax
import jax.numpy as jnp
from jax import lax
from jax.experimental import pallas as pl
from jax.experimental.pallas import tpu as pltpu
from jax.sharding import PartitionSpec as P

MODES = 32
RAMP = 0.25
BOTH = ("gx", "gy")
F32, BF16 = jnp.float32, jnp.bfloat16


def position(x, y, z, core):
    return ((z * 4 + (y // 2) * 2 + core) * 8) + (y % 2) * 4 + x


def partners(move):
    places = [(x, y, z, c) for z in range(8) for y in range(4) for x in range(4) for c in range(2)]
    return [(position(*place), position(*move(*place))) for place in places]


CHIP = partners(lambda x, y, z, c: (x, y, z, 1 - c))
EXCHANGES = (
    (
        partners(lambda x, y, z, c: (x ^ 1, y, z, 1 - c)),
        partners(lambda x, y, z, c: (x ^ 2, y, z, c)),
        partners(lambda x, y, z, c: (x ^ 3, y, z, 1 - c)),
    ),
    (
        partners(lambda x, y, z, c: (x, y ^ 1, z, 1 - c)),
        partners(lambda x, y, z, c: (x, y ^ 2, z, c)),
        partners(lambda x, y, z, c: (x, y ^ 3, z, 1 - c)),
    ),
    (partners(lambda x, y, z, c: (x, y, z ^ 1, 1 - c)),),
    (partners(lambda x, y, z, c: (x, y, z ^ 3, 1 - c)),),
    (partners(lambda x, y, z, c: (x, y, z ^ 7, 1 - c)),),
)


def half_held():
    gx, gy = lax.axis_index("gx"), lax.axis_index("gy")
    return (gx // 4 + gx + gy // 4 + gy) & 1


def cosines(index, wave, total):
    turn = ((2 * index + 1) * wave) & (4 * total - 1)
    turn = jnp.where(turn > 2 * total, 4 * total - turn, turn)
    y = (total - turn).astype(F32) * F32(math.pi / (2 * total))
    square = y * y
    series = F32(1.0 / math.factorial(13))
    for power in (11, 9, 7, 5, 3, 1):
        sign = -1.0 if power % 4 == 3 else 1.0
        series = series * square + F32(sign / math.factorial(power))
    scale = jnp.where(wave == 0, F32(math.sqrt(1.0 / total)), F32(math.sqrt(2.0 / total)))
    return scale * (y * series)


def split(value):
    high = value.astype(BF16)
    return high, (value - high.astype(F32)).astype(BF16)


def iota(shape, dim):
    return lax.broadcasted_iota(jnp.int32, shape, dim)


def dot(a, b):
    return jnp.dot(a, b, preferred_element_type=F32)


CHUNK = 6


def analysis(
    levels, variables, nx, ny, p_hbm, f_hbm, mine_ref, other_ref, p_buf, f_buf, p_sem, f_sem, w_ref, out_ref
):
    rows, cols = p_hbm.shape[2], p_hbm.shape[3]
    fields = [(l, v) for l in range(levels) for v in range(variables)]
    copies = []
    for k, (l, v) in enumerate(fields):
        pair = (
            pltpu.make_async_copy(p_hbm.at[l, v], p_buf.at[k], p_sem.at[k]),
            pltpu.make_async_copy(f_hbm.at[l, v], f_buf.at[k], f_sem.at[k]),
        )
        for copy in pair:
            copy.start()
        copies.append(pair)

    row0 = lax.axis_index("gx") * rows
    col0 = lax.axis_index("gy") * cols
    wide = 4 * MODES
    table = cosines(col0 + iota((cols, wide), 0), iota((cols, wide), 1) & (MODES - 1), ny)
    high, low = split(table)
    w_ref[:, :wide] = high
    w_ref[:, wide:] = low
    table = cosines(row0 + iota((MODES, rows), 1), iota((MODES, rows), 0), nx)
    high, low = split(table)
    row_table = jnp.concatenate(
        [jnp.concatenate([high, high], axis=1), jnp.concatenate([low, low], axis=1)], axis=0
    )
    lane_group = iota((8, wide), 1) // MODES

    for start in range(0, len(fields), CHUNK):
        chunk = range(start, min(start + CHUNK, len(fields)))
        for k in chunk:
            for copy in copies[k]:
                copy.wait()
        highs, lows = zip(*(split(f_buf[k].astype(F32) - p_buf[k]) for k in chunk))
        both = dot(jnp.concatenate(highs + lows, axis=0), w_ref[...])
        both = both[: len(chunk) * rows] + both[len(chunk) * rows :]
        high, low = split(both[:, :wide] + both[:, wide:])
        high = [high[i * rows : (i + 1) * rows] for i in range(len(chunk))]
        low = [low[i * rows : (i + 1) * rows] for i in range(len(chunk))]
        for i in range(0, len(chunk), 2):
            parts = [jnp.concatenate(part[i : i + 2], axis=1) for part in (high, low)]
            both = dot(row_table, jnp.concatenate(parts, axis=0))
            coefs = both[:MODES] + both[MODES:]
            for j, k in enumerate(chunk[i : i + 2]):
                tile = coefs[:8, wide * j : wide * (j + 1)]
                for q in range(1, 4):
                    part = coefs[8 * q : 8 * q + 8, wide * j : wide * (j + 1)]
                    tile = jnp.where(lane_group == q, part, tile)
                out_ref[8 * k : 8 * k + 8, :] = tile
    half = out_ref.shape[0] // 2
    first, second = out_ref[:half, :], out_ref[half:, :]
    held = half_held() == 0
    mine_ref[...] = jnp.where(held, first, second)
    other_ref[...] = jnp.where(held, second, first)


def preparation(levels, nx, ny, level_ref, pbl_ref, weight_ref, r_ref, t_ref):
    rows, cols = pbl_ref.shape
    row0 = lax.axis_index("gx") * rows
    col0 = lax.axis_index("gy") * cols
    wide = 4 * MODES
    for l in range(levels):
        weight_ref[l] = 1.0 / (1.0 + jnp.exp(-(level_ref[l] - pbl_ref[...]) / F32(RAMP)))
    lane_group = iota((1, wide), 1) // MODES
    high, low = split(cosines(row0 + iota((rows, wide), 0), iota((rows, wide), 1) & (MODES - 1), nx))
    none = jnp.zeros_like(high)
    r_ref[...] = jnp.where(lane_group < 2, high, jnp.where(lane_group == 2, low, none))
    high, low = split(cosines(col0 + iota((MODES, cols), 1), iota((MODES, cols), 0), ny))
    t_ref[0:32, :] = high
    t_ref[32:64, :] = high
    t_ref[64:96, :] = low
    t_ref[96:128, :] = jnp.zeros_like(high)


def synthesis(
    levels, variables,
    strength_ref, mine_ref, other_ref, weight_ref, r_ref, t_ref, out_hbm, energy_ref, o_buf, o_sem, z_ref,
):
    wide = 4 * MODES
    lane_group = iota((1, wide), 1) // MODES
    held = half_held() == 0
    half = levels * variables // 2
    at = (iota((levels, variables), 0), iota((levels, variables), 1))
    energy = jnp.zeros((levels, variables), F32)
    fields = [(l, v) for l in range(levels) for v in range(variables)]
    for start in range(0, len(fields), 2):
        sides = []
        for k in (start, start + 1):
            l, v = fields[k]
            line = 8 * (k % half)
            ours, theirs = mine_ref[line : line + 8, :], other_ref[line : line + 8, :]
            tile = jnp.where(held, ours, theirs) if k < half else jnp.where(held, theirs, ours)
            total = jnp.sum(tile * tile) / F32(MODES * MODES)
            energy = jnp.where((at[0] == l) & (at[1] == v), total, energy)
            tile = tile * strength_ref[l, v]
            blocks = []
            for q in range(4):
                one = jnp.where(lane_group == q, tile, 0.0)
                one = one + pltpu.roll(one, MODES, 1)
                blocks.append(one + pltpu.roll(one, 2 * MODES, 1))
            high, low = split(jnp.concatenate(blocks, axis=0))
            sides.append(jnp.concatenate([high, low, high, jnp.zeros_like(high)], axis=0))
        both = dot(r_ref[...], jnp.concatenate(sides, axis=1))
        for i, k in enumerate((start, start + 1)):
            high, low = split(both[:, wide * i : wide * (i + 1)])
            z_ref[k] = jnp.where(lane_group == 1, low, high)
    energy_ref[...] = energy

    copies = []
    for k, (l, v) in enumerate(fields):
        o_buf[k] = (weight_ref[l] * dot(z_ref[k], t_ref[...])).astype(BF16)
        copies.append(pltpu.make_async_copy(o_buf.at[k], out_hbm.at[l, v], o_sem.at[k]))
        if k:
            copies[k - 1].start()
    copies[-1].start()
    for copy in copies:
        copy.wait()


def in_vmem(value):
    return pltpu.with_memory_space_constraint(value, pltpu.VMEM)


def per_device(prognostic_values, forcing_host_values, strength, level_height, pbl_height):
    levels, variables, rows, cols = prognostic_values.shape
    nx, ny = rows * lax.axis_size("gx"), cols * lax.axis_size("gy")
    count = levels * variables
    lines = 8 * count
    wide = 4 * MODES
    anywhere = pl.BlockSpec(memory_space=pl.ANY)
    vmem = pl.BlockSpec(memory_space=pltpu.VMEM)
    smem = pl.BlockSpec(memory_space=pltpu.SMEM)

    mine, other = pl.pallas_call(
        lambda *refs: analysis(levels, variables, nx, ny, *refs),
        name="analysis",
        out_shape=(pltpu.VMEM((lines // 2, wide), F32), pltpu.VMEM((lines // 2, wide), F32)),
        in_specs=[anywhere, anywhere],
        out_specs=(vmem, vmem),
        scratch_shapes=[
            pltpu.VMEM((count, rows, cols), F32),
            pltpu.VMEM((count, rows, cols), BF16),
            pltpu.SemaphoreType.DMA((count,)),
            pltpu.SemaphoreType.DMA((count,)),
            pltpu.VMEM((cols, 2 * wide), BF16),
            pltpu.VMEM((lines, wide), F32),
        ],
    )(prognostic_values, forcing_host_values)

    weight, row_table, col_table = pl.pallas_call(
        lambda *refs: preparation(levels, nx, ny, *refs),
        name="preparation",
        out_shape=(
            pltpu.VMEM((levels, rows, cols), F32),
            pltpu.VMEM((rows, wide), BF16),
            pltpu.VMEM((wide, cols), BF16),
        ),
        in_specs=[smem, vmem],
        out_specs=(vmem, vmem, vmem),
    )(level_height, in_vmem(pbl_height))

    held = mine + lax.ppermute(other, BOTH, CHIP)
    prepared = (weight, row_table, col_table)
    for at, exchange in enumerate(EXCHANGES):
        if at == len(EXCHANGES) - 1:
            held, prepared = lax.optimization_barrier((held, prepared))
        held = sum((lax.ppermute(held, BOTH, pairs) for pairs in exchange), held)
    other = lax.ppermute(held, BOTH, CHIP)

    tendency, energy = pl.pallas_call(
        lambda *refs: synthesis(levels, variables, *refs),
        name="synthesis",
        out_shape=(
            jax.ShapeDtypeStruct((levels, variables, rows, cols), BF16),
            jax.ShapeDtypeStruct((levels, variables), F32),
        ),
        in_specs=[smem, vmem, vmem, vmem, vmem, vmem],
        out_specs=(anywhere, vmem),
        scratch_shapes=[
            pltpu.VMEM((count, rows, cols), BF16),
            pltpu.SemaphoreType.DMA((count,)),
            pltpu.VMEM((count, rows, wide), BF16),
        ],
    )(strength, in_vmem(held), in_vmem(other), *map(in_vmem, prepared))
    return tendency, energy


def solution(mesh):
    return jax.shard_map(
        per_device,
        mesh=mesh,
        in_specs=(P(None, None, "gx", "gy"), P(None, None, "gx", "gy"), P(), P(), P("gx", "gy")),
        out_specs=(P(None, None, "gx", "gy"), P()),
        check_vma=False,
    )
```

time: 59 us -> 44.6 us (0.76)
  blocking collectives: 42.3 us -> 0 us
  starting transfers between devices: 0 us -> 22.8 us
  waiting for transfers between devices: 0 us -> 11.5 us
  Pallas kernels: 15.5 us -> 9.43 us
    all_to_all x3 -> x0, blocking collectives: 42.3 us -> none  [the longest x1 18.9 us: per_device(): got = lax.all_to_all(share, BOTH, 0, 0, tiled=True, axis_index_groups=FAR)]
    ppermute x0 -> x11, starting transfers between devices: none -> 22.8 us  [the longest x9 19 us: per_device(): held = sum((lax.ppermute(held, BOTH, pairs) for pairs in exchange), held)]
    ppermute x0 -> x11, waiting for transfers between devices: none -> 11.5 us  [the longest x9 9.79 us: per_device(): held = sum((lax.ppermute(held, BOTH, pairs) for pairs in exchange), held)]
    pallas_call x2 -> x3, Pallas kernels: 15.5 us -> 9.43 us  [the longest x1 5.01 us: per_device(): pl.pallas_call(lambda *refs: analysis(levels, variables, nx, ny, *refs),...]
  transfers between devices with their start and end apart: 0 -> 11, of which waited for: 0 -> 10; matrix products, arithmetic and copies ran while one was open for 0% -> 0% of each run, Pallas kernels for 0% -> 2%
where the time goes in v2:
time: 44.6 us; the launch traced here: 44.4 us
  starting transfers between devices  22.8 us (51%)
  waiting for transfers between devices  11.5 us (26%)
  Pallas kernels  9.43 us (21%)
  between operations  0.67 us (2%)
    ppermute x9, starting transfers between devices, per_device(): held = sum((lax.ppermute(held, BOTH, pairs) for pairs in exchange), held)  19 us
    ppermute x9, waiting for transfers between devices, per_device(): held = sum((lax.ppermute(held, BOTH, pairs) for pairs in exchange), held)  9.79 us
    pallas_call x1, Pallas kernels, per_device(): pl.pallas_call(lambda *refs: analysis(levels, variables, nx, ny, *refs),...  5.01 us
    pallas_call x1, Pallas kernels, per_device(): pl.pallas_call(lambda *refs: synthesis(levels, variables, *refs), name='s...  3.44 us
    ppermute x1, starting transfers between devices, per_device(): held = mine + lax.ppermute(other, BOTH, CHIP)  3.29 us
    pallas_call x1, Pallas kernels, per_device(): pl.pallas_call(lambda *refs: preparation(levels, nx, ny, *refs), name='pr...  0.98 us
  transfers between devices with their start and end apart: 11, of which 10 were waited for; matrix products, arithmetic and copies ran while one was open for 0% of the time, Pallas kernels for 2%

profile of v2, /device:TPU:1, one launch (start us, length us, event | category | flops | bytes accessed | tf_op | source)
XLA Modules:
  0.0 44.4 jit_solution(16240062373489219102)
XLA Ops:
  0.6 5.0 %analysis.1 = (f32[72,128]{1,0:T(8,128)S(1)}, f32[72,128]{1,0:T(8,128)S(1)}) custom-call(f32[3,6,128,512]{3,2,1,0:T(8,128)} %refs_0_.3, bf16[3,6,128,512]{3,2,1,0:T(8,128)(2,1)} %refs_1_.2), custom_call_target="tpu_custom_call" | custom-call | tf_op jit(solution)/shard_map/analysis/pallas_call | solution.py:211
  5.7 3.3 %collective-permute-start = (f32[72,128]{1,0:T(8,128)S(1)}, f32[72,128]{1,0:T(8,128)S(1)}, u32[]{:S(2)}, u32[]{:S(2)}) collective-permute-start(f32[72,128]{1,0:T(8,128)S(1)} %get-tuple-element.12), channel_id=1, source_target_pairs={{0,8},{8,0},{1,9},{9,1},{2,10},{10,2},{3,11},{11,3},{4,12},{12,4},... | collective-permute-start | bytes 110600 | tf_op jit(solution)/shard_map/ppermute | solution.py:239
  8.9 0.9 %collective-permute-done = f32[72,128]{1,0:T(8,128)S(1)} collective-permute-done((f32[72,128]{1,0:T(8,128)S(1)}, f32[72,128]{1,0:T(8,128)S(1)}, u32[]{:S(2)}, u32[]{:S(2)}) %collective-permute-start) | collective-permute-done | bytes 36896 | tf_op jit(solution)/shard_map/ppermute | solution.py:239
  9.8 1.0 %collective-permute-start.3 = (f32[72,128]{1,0:T(8,128)S(1)}, f32[72,128]{1,0:T(8,128)S(1)}, u32[]{:S(2)}, u32[]{:S(2)}) collective-permute-start(f32[72,128]{1,0:T(8,128)S(1)} %add.30), channel_id=1, source_target_pairs={{0,11},{8,3},{1,10},{9,2},{2,9},{10,1},{3,8},{11,0},{4,15},{12,7},... | collective-permute-start | bytes 110600 | tf_op jit(solution)/shard_map/ppermute | solution.py:244
  10.8 0.5 %collective-permute-start.2 = (f32[72,128]{1,0:T(8,128)S(1)}, f32[72,128]{1,0:T(8,128)S(1)}, u32[]{:S(2)}, u32[]{:S(2)}) collective-permute-start(f32[72,128]{1,0:T(8,128)S(1)} %add.30), channel_id=1, source_target_pairs={{0,2},{8,10},{1,3},{9,11},{2,0},{10,8},{3,1},{11,9},{4,6},{12,14},... | collective-permute-start | bytes 110600 | tf_op jit(solution)/shard_map/ppermute | solution.py:244
  11.3 2.3 %collective-permute-start.1 = (f32[72,128]{1,0:T(8,128)S(1)}, f32[72,128]{1,0:T(8,128)S(1)}, u32[]{:S(2)}, u32[]{:S(2)}) collective-permute-start(f32[72,128]{1,0:T(8,128)S(1)} %add.30), channel_id=1, source_target_pairs={{0,9},{8,1},{1,8},{9,0},{2,11},{10,3},{3,10},{11,2},{4,13},{12,5},... | collective-permute-start | bytes 110600 | tf_op jit(solution)/shard_map/ppermute | solution.py:244
  13.6 0.8 %collective-permute-done.3 = f32[72,128]{1,0:T(8,128)S(1)} collective-permute-done((f32[72,128]{1,0:T(8,128)S(1)}, f32[72,128]{1,0:T(8,128)S(1)}, u32[]{:S(2)}, u32[]{:S(2)}) %collective-permute-start.3) | collective-permute-done | bytes 36896 | tf_op jit(solution)/shard_map/ppermute | solution.py:244
  14.5 0.7 %collective-permute-done.2 = f32[72,128]{1,0:T(8,128)S(1)} collective-permute-done((f32[72,128]{1,0:T(8,128)S(1)}, f32[72,128]{1,0:T(8,128)S(1)}, u32[]{:S(2)}, u32[]{:S(2)}) %collective-permute-start.2) | collective-permute-done | bytes 36896 | tf_op jit(solution)/shard_map/ppermute | solution.py:244
  15.1 1.0 %collective-permute-done.1 = f32[72,128]{1,0:T(8,128)S(1)} collective-permute-done((f32[72,128]{1,0:T(8,128)S(1)}, f32[72,128]{1,0:T(8,128)S(1)}, u32[]{:S(2)}, u32[]{:S(2)}) %collective-permute-start.1) | collective-permute-done | bytes 36896 | tf_op jit(solution)/shard_map/ppermute | solution.py:244
  16.1 3.2 %collective-permute-start.6 = (f32[72,128]{1,0:T(8,128)S(1)}, f32[72,128]{1,0:T(8,128)S(1)}, u32[]{:S(2)}, u32[]{:S(2)}) collective-permute-start(f32[72,128]{1,0:T(8,128)S(1)} %add_add_fusion.1), channel_id=1, source_target_pairs={{0,28},{8,20},{1,29},{9,21},{2,30},{10,22},{3,31},{11,23},{4,24},{... | collective-permute-start | bytes 110600 | tf_op jit(solution)/shard_map/ppermute | solution.py:244
  19.3 0.4 collective-permute-start.5
  19.7 0.6 %collective-permute-start.4 = (f32[72,128]{1,0:T(8,128)S(1)}, f32[72,128]{1,0:T(8,128)S(1)}, u32[]{:S(2)}, u32[]{:S(2)}) collective-permute-start(f32[72,128]{1,0:T(8,128)S(1)} %add_add_fusion.1), channel_id=1, source_target_pairs={{0,12},{8,4},{1,13},{9,5},{2,14},{10,6},{3,15},{11,7},{4,8},{12,0}... | collective-permute-start | bytes 110600 | tf_op jit(solution)/shard_map/ppermute | solution.py:244
  20.3 0.7 %collective-permute-done.6 = f32[72,128]{1,0:T(8,128)S(1)} collective-permute-done((f32[72,128]{1,0:T(8,128)S(1)}, f32[72,128]{1,0:T(8,128)S(1)}, u32[]{:S(2)}, u32[]{:S(2)}) %collective-permute-start.6) | collective-permute-done | bytes 36896 | tf_op jit(solution)/shard_map/ppermute | solution.py:244
  21.0 2.6 %collective-permute-done.5 = f32[72,128]{1,0:T(8,128)S(1)} collective-permute-done((f32[72,128]{1,0:T(8,128)S(1)}, f32[72,128]{1,0:T(8,128)S(1)}, u32[]{:S(2)}, u32[]{:S(2)}) %collective-permute-start.5) | collective-permute-done | bytes 36896 | tf_op jit(solution)/shard_map/ppermute | solution.py:244
  23.6 1.9 %collective-permute-start.7 = (f32[72,128]{1,0:T(8,128)S(1)}, f32[72,128]{1,0:T(8,128)S(1)}, u32[]{:S(2)}, u32[]{:S(2)}) collective-permute-start(f32[72,128]{1,0:T(8,128)S(1)} %add_add_fusion), channel_id=1, source_target_pairs={{0,40},{8,32},{1,41},{9,33},{2,42},{10,34},{3,43},{11,35},{4,44},{... | collective-permute-start | bytes 110600 | tf_op jit(solution)/shard_map/ppermute | solution.py:244
  25.5 1.6 %collective-permute-done.7 = f32[72,128]{1,0:T(8,128)S(1)} collective-permute-done((f32[72,128]{1,0:T(8,128)S(1)}, f32[72,128]{1,0:T(8,128)S(1)}, u32[]{:S(2)}, u32[]{:S(2)}) %collective-permute-start.7) | collective-permute-done | bytes 36896 | tf_op jit(solution)/shard_map/ppermute | solution.py:244
  27.1 4.4 %collective-permute-start.8 = (f32[72,128]{1,0:T(8,128)S(1)}, f32[72,128]{1,0:T(8,128)S(1)}, u32[]{:S(2)}, u32[]{:S(2)}) collective-permute-start(f32[72,128]{1,0:T(8,128)S(1)} %add.37), channel_id=1, source_target_pairs={{0,104},{8,96},{1,105},{9,97},{2,106},{10,98},{3,107},{11,99},{4,1... | collective-permute-start | bytes 110600 | tf_op jit(solution)/shard_map/ppermute | solution.py:244
  31.6 1.0 %preparation.1 = (f32[3,128,512]{2,1,0:T(8,128)S(1)}, bf16[128,128]{1,0:T(8,128)(2,1)S(1)}, bf16[128,512]{1,0:T(8,128)(2,1)S(1)}) custom-call(f32[3]{0:T(128)} %refs_0_.4, f32[128,512]{1,0:T(8,128)S(1)} %copy-done), custom_call_target="tpu_custom_call" | custom-call | tf_op jit(solution)/shard_map/preparation/pallas_call | solution.py:227
  32.6 0.7 %collective-permute-done.8 = f32[72,128]{1,0:T(8,128)S(1)} collective-permute-done((f32[72,128]{1,0:T(8,128)S(1)}, f32[72,128]{1,0:T(8,128)S(1)}, u32[]{:S(2)}, u32[]{:S(2)}) %collective-permute-start.8) | collective-permute-done | bytes 36896 | tf_op jit(solution)/shard_map/ppermute | solution.py:244
  33.2 4.8 %collective-permute-start.9 = (f32[72,128]{1,0:T(8,128)S(1)}, f32[72,128]{1,0:T(8,128)S(1)}, u32[]{:S(2)}, u32[]{:S(2)}) collective-permute-start(f32[72,128]{1,0:T(8,128)S(1)} %add.38), channel_id=1, source_target_pairs={{0,232},{8,224},{1,233},{9,225},{2,234},{10,226},{3,235},{11,227},... | collective-permute-start | bytes 110600 | tf_op jit(solution)/shard_map/ppermute | solution.py:244
  38.0 1.6 %collective-permute-done.9 = f32[72,128]{1,0:T(8,128)S(1)} collective-permute-done((f32[72,128]{1,0:T(8,128)S(1)}, f32[72,128]{1,0:T(8,128)S(1)}, u32[]{:S(2)}, u32[]{:S(2)}) %collective-permute-start.9) | collective-permute-done | bytes 36896 | tf_op jit(solution)/shard_map/ppermute | solution.py:244
  39.7 0.5 %collective-permute-start.10 = (f32[72,128]{1,0:T(8,128)S(1)}, f32[72,128]{1,0:T(8,128)S(1)}, u32[]{:S(2)}, u32[]{:S(2)}) collective-permute-start(f32[72,128]{1,0:T(8,128)S(1)} %add.39.refs_1_), channel_id=1, source_target_pairs={{0,8},{8,0},{1,9},{9,1},{2,10},{10,2},{3,11},{11,3},{4,12},{12,4},... | collective-permute-start | bytes 110600 | tf_op jit(solution)/shard_map/ppermute | solution.py:245
  40.1 0.9 %collective-permute-done.10.refs_2_ = f32[72,128]{1,0:T(8,128)S(1)} collective-permute-done((f32[72,128]{1,0:T(8,128)S(1)}, f32[72,128]{1,0:T(8,128)S(1)}, u32[]{:S(2)}, u32[]{:S(2)}) %collective-permute-start.10) | collective-permute-done | bytes 36896 | tf_op jit(solution)/shard_map/ppermute | solution.py:245
  41.0 3.4 %synthesis.1 = (bf16[3,6,128,512]{3,2,1,0:T(8,128)(2,1)}, f32[3,6]{1,0:T(4,128)}) custom-call(f32[3,6]{1,0:T(4,128)} %refs_0_.5, f32[72,128]{1,0:T(8,128)S(1)} %add.39.refs_1_, f32[72,128]{1,0:T(8,128)S(1)} %collective-permute-done.10.refs_2_, f32[3,128,512]{2,1,0:T(8,128)S(1)} %get-tuple-element.17.refs_3_, bf16[128,128]{1,0:T(8,128)(2,1)S(1)} %get-tuple-element.18.refs_4_, ...), custom_call_target="tpu_custom_call" | custom-call | tf_op jit(solution)/shard_map/synthesis/pallas_call | solution.py:247
  (9 shorter events, 0.1 us)
Async XLA Ops:
  0.6 31.0 %copy-start = (f32[128,512]{1,0:T(8,128)S(1)}, f32[128,512]{1,0:T(8,128)}, u32[]{:S(2)}) copy-start(f32[128,512]{1,0:T(8,128)} %refs_1_.3) | copy-start | bytes 786436
  5.7 4.2 %collective-permute-start = (f32[72,128]{1,0:T(8,128)S(1)}, f32[72,128]{1,0:T(8,128)S(1)}, u32[]{:S(2)}, u32[]{:S(2)}) collective-permute-start(f32[72,128]{1,0:T(8,128)S(1)} %get-tuple-element.12), channel_id=1, source_target_pairs={{0,8},{8,0},{1,9},{9,1},{2,10},{10,2},{3,11},{11,3},{4,12},{12,4},... | collective-permute-start | bytes 110600 | tf_op jit(solution)/shard_map/ppermute | solution.py:239
  9.8 4.6 %collective-permute-start.3 = (f32[72,128]{1,0:T(8,128)S(1)}, f32[72,128]{1,0:T(8,128)S(1)}, u32[]{:S(2)}, u32[]{:S(2)}) collective-permute-start(f32[72,128]{1,0:T(8,128)S(1)} %add.30), channel_id=1, source_target_pairs={{0,11},{8,3},{1,10},{9,2},{2,9},{10,1},{3,8},{11,0},{4,15},{12,7},... | collective-permute-start | bytes 110600 | tf_op jit(solution)/shard_map/ppermute | solution.py:244
  10.8 4.3 %collective-permute-start.2 = (f32[72,128]{1,0:T(8,128)S(1)}, f32[72,128]{1,0:T(8,128)S(1)}, u32[]{:S(2)}, u32[]{:S(2)}) collective-permute-start(f32[72,128]{1,0:T(8,128)S(1)} %add.30), channel_id=1, source_target_pairs={{0,2},{8,10},{1,3},{9,11},{2,0},{10,8},{3,1},{11,9},{4,6},{12,14},... | collective-permute-start | bytes 110600 | tf_op jit(solution)/shard_map/ppermute | solution.py:244
  11.3 4.8 %collective-permute-start.1 = (f32[72,128]{1,0:T(8,128)S(1)}, f32[72,128]{1,0:T(8,128)S(1)}, u32[]{:S(2)}, u32[]{:S(2)}) collective-permute-start(f32[72,128]{1,0:T(8,128)S(1)} %add.30), channel_id=1, source_target_pairs={{0,9},{8,1},{1,8},{9,0},{2,11},{10,3},{3,10},{11,2},{4,13},{12,5},... | collective-permute-start | bytes 110600 | tf_op jit(solution)/shard_map/ppermute | solution.py:244
  16.1 4.8 %collective-permute-start.6 = (f32[72,128]{1,0:T(8,128)S(1)}, f32[72,128]{1,0:T(8,128)S(1)}, u32[]{:S(2)}, u32[]{:S(2)}) collective-permute-start(f32[72,128]{1,0:T(8,128)S(1)} %add_add_fusion.1), channel_id=1, source_target_pairs={{0,28},{8,20},{1,29},{9,21},{2,30},{10,22},{3,31},{11,23},{4,24},{... | collective-permute-start | bytes 110600 | tf_op jit(solution)/shard_map/ppermute | solution.py:244
  19.3 4.3 %collective-permute-start.5 = (f32[72,128]{1,0:T(8,128)S(1)}, f32[72,128]{1,0:T(8,128)S(1)}, u32[]{:S(2)}, u32[]{:S(2)}) collective-permute-start(f32[72,128]{1,0:T(8,128)S(1)} %add_add_fusion.1), channel_id=1, source_target_pairs={{0,16},{8,24},{1,17},{9,25},{2,18},{10,26},{3,19},{11,27},{4,20},{... | collective-permute-start | bytes 110600 | tf_op jit(solution)/shard_map/ppermute | solution.py:244
  19.7 4.0 %collective-permute-start.4 = (f32[72,128]{1,0:T(8,128)S(1)}, f32[72,128]{1,0:T(8,128)S(1)}, u32[]{:S(2)}, u32[]{:S(2)}) collective-permute-start(f32[72,128]{1,0:T(8,128)S(1)} %add_add_fusion.1), channel_id=1, source_target_pairs={{0,12},{8,4},{1,13},{9,5},{2,14},{10,6},{3,15},{11,7},{4,8},{12,0}... | collective-permute-start | bytes 110600 | tf_op jit(solution)/shard_map/ppermute | solution.py:244
  23.6 3.5 %collective-permute-start.7 = (f32[72,128]{1,0:T(8,128)S(1)}, f32[72,128]{1,0:T(8,128)S(1)}, u32[]{:S(2)}, u32[]{:S(2)}) collective-permute-start(f32[72,128]{1,0:T(8,128)S(1)} %add_add_fusion), channel_id=1, source_target_pairs={{0,40},{8,32},{1,41},{9,33},{2,42},{10,34},{3,43},{11,35},{4,44},{... | collective-permute-start | bytes 110600 | tf_op jit(solution)/shard_map/ppermute | solution.py:244
  27.1 6.1 %collective-permute-start.8 = (f32[72,128]{1,0:T(8,128)S(1)}, f32[72,128]{1,0:T(8,128)S(1)}, u32[]{:S(2)}, u32[]{:S(2)}) collective-permute-start(f32[72,128]{1,0:T(8,128)S(1)} %add.37), channel_id=1, source_target_pairs={{0,104},{8,96},{1,105},{9,97},{2,106},{10,98},{3,107},{11,99},{4,1... | collective-permute-start | bytes 110600 | tf_op jit(solution)/shard_map/ppermute | solution.py:244
  33.2 6.4 %collective-permute-start.9 = (f32[72,128]{1,0:T(8,128)S(1)}, f32[72,128]{1,0:T(8,128)S(1)}, u32[]{:S(2)}, u32[]{:S(2)}) collective-permute-start(f32[72,128]{1,0:T(8,128)S(1)} %add.38), channel_id=1, source_target_pairs={{0,232},{8,224},{1,233},{9,225},{2,234},{10,226},{3,235},{11,227},... | collective-permute-start | bytes 110600 | tf_op jit(solution)/shard_map/ppermute | solution.py:244
  39.7 1.3 %collective-permute-start.10 = (f32[72,128]{1,0:T(8,128)S(1)}, f32[72,128]{1,0:T(8,128)S(1)}, u32[]{:S(2)}, u32[]{:S(2)}) collective-permute-start(f32[72,128]{1,0:T(8,128)S(1)} %add.39.refs_1_), channel_id=1, source_target_pairs={{0,8},{8,0},{1,9},{9,1},{2,10},{10,2},{3,11},{11,3},{4,12},{12,4},... | collective-permute-start | bytes 110600 | tf_op jit(solution)/shard_map/ppermute | solution.py:245

commit v3 on v2

v3 whole, which is shorter than its diff:
```python
import math

import jax
import jax.numpy as jnp
from jax import lax
from jax.experimental import pallas as pl
from jax.experimental.pallas import tpu as pltpu
from jax.sharding import PartitionSpec as P

MODES = 32
RAMP = 0.25
BOTH = ("gx", "gy")
F32, BF16 = jnp.float32, jnp.bfloat16


def position(x, y, z, core):
    return ((z * 4 + (y // 2) * 2 + core) * 8) + (y % 2) * 4 + x


def partners(move):
    places = [(x, y, z, c) for z in range(8) for y in range(4) for x in range(4) for c in range(2)]
    return [(position(*place), position(*move(*place))) for place in places]


CHIP = partners(lambda x, y, z, c: (x, y, z, 1 - c))
EXCHANGES = (
    (
        partners(lambda x, y, z, c: (x ^ 1, y, z, 1 - c)),
        partners(lambda x, y, z, c: (x ^ 2, y, z, c)),
        partners(lambda x, y, z, c: (x ^ 3, y, z, 1 - c)),
    ),
    (
        partners(lambda x, y, z, c: (x, y ^ 1, z, 1 - c)),
        partners(lambda x, y, z, c: (x, y ^ 2, z, c)),
        partners(lambda x, y, z, c: (x, y ^ 3, z, 1 - c)),
    ),
    (partners(lambda x, y, z, c: (x, y, z ^ 1, 1 - c)),),
    (partners(lambda x, y, z, c: (x, y, z ^ 3, 1 - c)),),
    (partners(lambda x, y, z, c: (x, y, z ^ 7, 1 - c)),),
)


def half_held():
    gx, gy = lax.axis_index("gx"), lax.axis_index("gy")
    return (gx // 4 + gx + gy // 4 + gy) & 1


def cosines(index, wave, total):
    turn = ((2 * index + 1) * wave) & (4 * total - 1)
    turn = jnp.where(turn > 2 * total, 4 * total - turn, turn)
    y = (total - turn).astype(F32) * F32(math.pi / (2 * total))
    square = y * y
    series = F32(1.0 / math.factorial(13))
    for power in (11, 9, 7, 5, 3, 1):
        sign = -1.0 if power % 4 == 3 else 1.0
        series = series * square + F32(sign / math.factorial(power))
    scale = jnp.where(wave == 0, F32(math.sqrt(1.0 / total)), F32(math.sqrt(2.0 / total)))
    return scale * (y * series)


def split(value):
    high = value.astype(BF16)
    return high, (value - high.astype(F32)).astype(BF16)


def iota(shape, dim):
    return lax.broadcasted_iota(jnp.int32, shape, dim)


def dot(a, b):
    return jnp.dot(a, b, preferred_element_type=F32)


CHUNK = 6


def analysis(
    count, nx, ny, p_hbm, f_hbm, mine_ref, other_ref, p_buf, f_buf, p_sem, f_sem, w_ref, out_ref
):
    rows, cols = p_hbm.shape[1:]
    copies = []
    for at, start in enumerate(range(0, count, CHUNK)):
        chunk = pl.ds(start, CHUNK)
        pair = (
            pltpu.make_async_copy(p_hbm.at[chunk], p_buf.at[chunk], p_sem.at[at]),
            pltpu.make_async_copy(f_hbm.at[chunk], f_buf.at[chunk], f_sem.at[at]),
        )
        for copy in pair:
            copy.start()
        copies.append(pair)

    row0 = lax.axis_index("gx") * rows
    col0 = lax.axis_index("gy") * cols
    wide = 4 * MODES
    table = cosines(col0 + iota((cols, wide), 0), iota((cols, wide), 1) & (MODES - 1), ny)
    high, low = split(table)
    w_ref[:, :wide] = high
    w_ref[:, wide:] = low
    table = cosines(row0 + iota((MODES, rows), 1), iota((MODES, rows), 0), nx)
    high, low = split(table)
    row_table = jnp.concatenate(
        [jnp.concatenate([high, high], axis=1), jnp.concatenate([low, low], axis=1)], axis=0
    )
    lane_group = iota((8, wide), 1) // MODES

    for pair, start in zip(copies, range(0, count, CHUNK)):
        for copy in pair:
            copy.wait()
        parts = []
        for k in range(start, start + CHUNK):
            diff = jnp.concatenate(split(f_buf[k].astype(F32) - p_buf[k]), axis=0)
            both = dot(row_table, diff)
            parts.append(both[:MODES] + both[MODES:])
        part = jnp.concatenate(split(jnp.concatenate(parts, axis=0)), axis=0)
        both = dot(part, w_ref[...])
        both = both[: CHUNK * MODES] + both[CHUNK * MODES :]
        both = both[:, :wide] + both[:, wide:]
        for i in range(CHUNK):
            coefs = both[MODES * i : MODES * (i + 1)]
            tile = coefs[:8]
            for q in range(1, 4):
                tile = jnp.where(lane_group == q, coefs[8 * q : 8 * q + 8], tile)
            line = 8 * (start + i)
            out_ref[line : line + 8, :] = tile
    half = out_ref.shape[0] // 2
    first, second = out_ref[:half, :], out_ref[half:, :]
    held = half_held() == 0
    mine_ref[...] = jnp.where(held, first, second)
    other_ref[...] = jnp.where(held, second, first)


def preparation(
    levels, variables, nx, ny, strength_ref, level_ref, pbl_ref, weight_ref, r_ref, t_ref, scale_ref
):
    rows, cols = pbl_ref.shape
    row0 = lax.axis_index("gx") * rows
    col0 = lax.axis_index("gy") * cols
    wide = 4 * MODES
    for l in range(levels):
        weight_ref[l] = 1.0 / (1.0 + jnp.exp(-(level_ref[l] - pbl_ref[...]) / F32(RAMP)))
        for v in range(variables):
            scale_ref[l * variables + v] = jnp.full((8, wide), strength_ref[l, v], F32)
    lane_group = iota((1, wide), 1) // MODES
    high, low = split(cosines(row0 + iota((rows, wide), 0), iota((rows, wide), 1) & (MODES - 1), nx))
    none = jnp.zeros_like(high)
    r_ref[...] = jnp.where(lane_group < 2, high, jnp.where(lane_group == 2, low, none))
    high, low = split(cosines(col0 + iota((MODES, cols), 1), iota((MODES, cols), 0), ny))
    t_ref[0:32, :] = high
    t_ref[32:64, :] = high
    t_ref[64:96, :] = low
    t_ref[96:128, :] = jnp.zeros_like(high)


AHEAD = 6


def synthesis(
    levels, variables,
    mine_ref, other_ref, weight_ref, r_ref, t_ref, scale_ref,
    out_hbm, energy_hbm, o_buf, o_sem, z_ref, e_ref, e_sem,
):
    count = levels * variables
    wide = 4 * MODES
    lane_group = iota((1, wide), 1) // MODES
    held = half_held() == 0
    half = count // 2
    tiles = []
    for k in range(count):
        line = 8 * (k % half)
        ours, theirs = mine_ref[line : line + 8, :], other_ref[line : line + 8, :]
        tiles.append(jnp.where(held, ours, theirs) if k < half else jnp.where(held, theirs, ours))

    def rows_of(start):
        sides = []
        for k in (start, start + 1):
            tile = tiles[k] * scale_ref[k]
            blocks = []
            for q in range(4):
                one = jnp.where(lane_group == q, tile, 0.0)
                one = one + pltpu.roll(one, MODES, 1)
                blocks.append(one + pltpu.roll(one, 2 * MODES, 1))
            high, low = split(jnp.concatenate(blocks, axis=0))
            sides.append(jnp.concatenate([high, low, high, jnp.zeros_like(high)], axis=0))
        both = dot(r_ref[...], jnp.concatenate(sides, axis=1))
        for i, k in enumerate((start, start + 1)):
            high, low = split(both[:, wide * i : wide * (i + 1)])
            z_ref[k] = jnp.where(lane_group == 1, low, high)

    for start in range(0, AHEAD, 2):
        rows_of(start)
    at = (iota((levels, variables), 0), iota((levels, variables), 1))
    energy = jnp.zeros((levels, variables), F32)
    for k, tile in enumerate(tiles):
        here = (at[0] == k // variables) & (at[1] == k % variables)
        energy = jnp.where(here, jnp.sum(tile * tile) / F32(MODES * MODES), energy)
    e_ref[...] = energy

    copies = [pltpu.make_async_copy(e_ref, energy_hbm, e_sem)]
    for k in range(count):
        if k % 2 == 0 and k + AHEAD < count:
            rows_of(k + AHEAD)
        o_buf[k] = (weight_ref[k // variables] * dot(z_ref[k], t_ref[...])).astype(BF16)
        copies[k].start()
        copies.append(pltpu.make_async_copy(o_buf.at[k], out_hbm.at[k], o_sem.at[k]))
    copies[-1].start()
    for copy in copies:
        copy.wait()


def in_vmem(value):
    return pltpu.with_memory_space_constraint(value, pltpu.VMEM)


def total(parts):
    while len(parts) > 1:
        parts = [a + b for a, b in zip(parts[::2], parts[1::2])]
    return parts[0]


def per_device(prognostic_values, forcing_host_values, strength, level_height, pbl_height):
    levels, variables, rows, cols = prognostic_values.shape
    nx, ny = rows * lax.axis_size("gx"), cols * lax.axis_size("gy")
    count = levels * variables
    lines = 8 * count
    wide = 4 * MODES
    anywhere = pl.BlockSpec(memory_space=pl.ANY)
    vmem = pl.BlockSpec(memory_space=pltpu.VMEM)
    smem = pl.BlockSpec(memory_space=pltpu.SMEM)

    mine, other = pl.pallas_call(
        lambda *refs: analysis(count, nx, ny, *refs),
        name="analysis",
        out_shape=(pltpu.VMEM((lines // 2, wide), F32), pltpu.VMEM((lines // 2, wide), F32)),
        in_specs=[anywhere, anywhere],
        out_specs=(vmem, vmem),
        scratch_shapes=[
            pltpu.VMEM((count, rows, cols), F32),
            pltpu.VMEM((count, rows, cols), BF16),
            pltpu.SemaphoreType.DMA((count // CHUNK,)),
            pltpu.SemaphoreType.DMA((count // CHUNK,)),
            pltpu.VMEM((cols, 2 * wide), BF16),
            pltpu.VMEM((lines, wide), F32),
        ],
    )(prognostic_values.reshape(count, rows, cols), forcing_host_values.reshape(count, rows, cols))

    prepared = pl.pallas_call(
        lambda *refs: preparation(levels, variables, nx, ny, *refs),
        name="preparation",
        out_shape=(
            pltpu.VMEM((levels, rows, cols), F32),
            pltpu.VMEM((rows, wide), BF16),
            pltpu.VMEM((wide, cols), BF16),
            pltpu.VMEM((count, 8, wide), F32),
        ),
        in_specs=[smem, smem, vmem],
        out_specs=(vmem, vmem, vmem, vmem),
    )(strength, level_height, in_vmem(pbl_height))

    held = mine + lax.ppermute(other, BOTH, CHIP)
    for at, exchange in enumerate(EXCHANGES):
        if at == len(EXCHANGES) - 1:
            held, prepared = lax.optimization_barrier((held, prepared))
        held = total([held] + [lax.ppermute(held, BOTH, pairs) for pairs in exchange])
    other = lax.ppermute(held, BOTH, CHIP)

    tendency, energy = pl.pallas_call(
        lambda *refs: synthesis(levels, variables, *refs),
        name="synthesis",
        out_shape=(
            jax.ShapeDtypeStruct((count, rows, cols), BF16),
            jax.ShapeDtypeStruct((levels, variables), F32),
        ),
        in_specs=[vmem] * 6,
        out_specs=(anywhere, anywhere),
        scratch_shapes=[
            pltpu.VMEM((count, rows, cols), BF16),
            pltpu.SemaphoreType.DMA((count,)),
            pltpu.VMEM((count, rows, wide), BF16),
            pltpu.VMEM((levels, variables), F32),
            pltpu.SemaphoreType.DMA,
        ],
    )(in_vmem(held), in_vmem(other), *map(in_vmem, prepared))
    return tendency.reshape(levels, variables, rows, cols), energy


def solution(mesh):
    return jax.shard_map(
        per_device,
        mesh=mesh,
        in_specs=(P(None, None, "gx", "gy"), P(None, None, "gx", "gy"), P(), P(), P("gx", "gy")),
        out_specs=(P(None, None, "gx", "gy"), P()),
        check_vma=False,
    )
```

time: 44.6 us -> 42 us (0.942)
  Pallas kernels: 9.43 us -> 6.89 us
    pallas_call x1, Pallas kernels: 3.44 us -> 2.12 us  [per_device(): pl.pallas_call(lambda *refs: synthesis(levels, variables, *refs), name='s...]
    pallas_call x2, Pallas kernels: 5.99 us -> 4.78 us  [the longest x1 3.76 us: per_device(): pl.pallas_call(lambda *refs: analysis(count, nx, ny, *refs), name='analys...]
where the time goes in v3:
time: 42 us; the launch traced here: 41.9 us
  starting transfers between devices  22.8 us (54%)
  waiting for transfers between devices  11.5 us (27%)
  Pallas kernels  6.89 us (16%)
  between operations  0.68 us (2%)
    ppermute x9, starting transfers between devices, per_device(): lax.ppermute(held, BOTH, pairs)  19 us
    ppermute x9, waiting for transfers between devices, per_device(): lax.ppermute(held, BOTH, pairs)  9.75 us
    pallas_call x1, Pallas kernels, per_device(): pl.pallas_call(lambda *refs: analysis(count, nx, ny, *refs), name='analys...  3.76 us
    ppermute x1, starting transfers between devices, per_device(): held = mine + lax.ppermute(other, BOTH, CHIP)  3.29 us
    pallas_call x1, Pallas kernels, per_device(): pl.pallas_call(lambda *refs: synthesis(levels, variables, *refs), name='s...  2.12 us
    pallas_call x1, Pallas kernels, per_device(): pl.pallas_call(lambda *refs: preparation(levels, variables, nx, ny, *refs...  1.02 us
    ppermute x1, waiting for transfers between devices, per_device(): held = mine + lax.ppermute(other, BOTH, CHIP)  0.87 us
    ppermute x1, waiting for transfers between devices, per_device(): other = lax.ppermute(held, BOTH, CHIP)  0.87 us
  transfers between devices with their start and end apart: 11, of which 10 were waited for; matrix products, arithmetic and copies ran while one was open for 0% of the time, Pallas kernels for 2%

profile of v3, /device:TPU:1, one launch (start us, length us, event | category | flops | bytes accessed | tf_op | source)
XLA Modules:
  0.0 41.9 jit_solution(10275795067749343933)
XLA Ops:
  0.6 3.8 %analysis.1 = (f32[72,128]{1,0:T(8,128)S(1)}, f32[72,128]{1,0:T(8,128)S(1)}) custom-call(f32[18,128,512]{2,1,0:T(8,128)} %bitcast.3, bf16[18,128,512]{2,1,0:T(8,128)(2,1)} %bitcast.4), custom_call_target="tpu_custom_call" | custom-call | tf_op jit(solution)/shard_map/analysis/pallas_call | solution.py:230
  4.4 3.3 %collective-permute-start = (f32[72,128]{1,0:T(8,128)S(1)}, f32[72,128]{1,0:T(8,128)S(1)}, u32[]{:S(2)}, u32[]{:S(2)}) collective-permute-start(f32[72,128]{1,0:T(8,128)S(1)} %get-tuple-element.16), channel_id=1, source_target_pairs={{0,8},{8,0},{1,9},{9,1},{2,10},{10,2},{3,11},{11,3},{4,12},{12,4},... | collective-permute-start | bytes 110600 | tf_op jit(solution)/shard_map/ppermute | solution.py:259
  7.7 0.9 %collective-permute-done = f32[72,128]{1,0:T(8,128)S(1)} collective-permute-done((f32[72,128]{1,0:T(8,128)S(1)}, f32[72,128]{1,0:T(8,128)S(1)}, u32[]{:S(2)}, u32[]{:S(2)}) %collective-permute-start) | collective-permute-done | bytes 36896 | tf_op jit(solution)/shard_map/ppermute | solution.py:259
  8.6 1.0 %collective-permute-start.3 = (f32[72,128]{1,0:T(8,128)S(1)}, f32[72,128]{1,0:T(8,128)S(1)}, u32[]{:S(2)}, u32[]{:S(2)}) collective-permute-start(f32[72,128]{1,0:T(8,128)S(1)} %add.30), channel_id=1, source_target_pairs={{0,11},{8,3},{1,10},{9,2},{2,9},{10,1},{3,8},{11,0},{4,15},{12,7},... | collective-permute-start | bytes 110600 | tf_op jit(solution)/shard_map/ppermute | solution.py:263
  9.6 0.5 %collective-permute-start.2 = (f32[72,128]{1,0:T(8,128)S(1)}, f32[72,128]{1,0:T(8,128)S(1)}, u32[]{:S(2)}, u32[]{:S(2)}) collective-permute-start(f32[72,128]{1,0:T(8,128)S(1)} %add.30), channel_id=1, source_target_pairs={{0,2},{8,10},{1,3},{9,11},{2,0},{10,8},{3,1},{11,9},{4,6},{12,14},... | collective-permute-start | bytes 110600 | tf_op jit(solution)/shard_map/ppermute | solution.py:263
  10.1 2.3 %collective-permute-start.1 = (f32[72,128]{1,0:T(8,128)S(1)}, f32[72,128]{1,0:T(8,128)S(1)}, u32[]{:S(2)}, u32[]{:S(2)}) collective-permute-start(f32[72,128]{1,0:T(8,128)S(1)} %add.30), channel_id=1, source_target_pairs={{0,9},{8,1},{1,8},{9,0},{2,11},{10,3},{3,10},{11,2},{4,13},{12,5},... | collective-permute-start | bytes 110600 | tf_op jit(solution)/shard_map/ppermute | solution.py:263
  12.4 0.8 %collective-permute-done.3 = f32[72,128]{1,0:T(8,128)S(1)} collective-permute-done((f32[72,128]{1,0:T(8,128)S(1)}, f32[72,128]{1,0:T(8,128)S(1)}, u32[]{:S(2)}, u32[]{:S(2)}) %collective-permute-start.3) | collective-permute-done | bytes 36896 | tf_op jit(solution)/shard_map/ppermute | solution.py:263
  13.2 0.7 %collective-permute-done.2 = f32[72,128]{1,0:T(8,128)S(1)} collective-permute-done((f32[72,128]{1,0:T(8,128)S(1)}, f32[72,128]{1,0:T(8,128)S(1)}, u32[]{:S(2)}, u32[]{:S(2)}) %collective-permute-start.2) | collective-permute-done | bytes 36896 | tf_op jit(solution)/shard_map/ppermute | solution.py:263
  13.9 1.0 %collective-permute-done.1 = f32[72,128]{1,0:T(8,128)S(1)} collective-permute-done((f32[72,128]{1,0:T(8,128)S(1)}, f32[72,128]{1,0:T(8,128)S(1)}, u32[]{:S(2)}, u32[]{:S(2)}) %collective-permute-start.1) | collective-permute-done | bytes 36896 | tf_op jit(solution)/shard_map/ppermute | solution.py:263
  14.9 3.2 %collective-permute-start.6 = (f32[72,128]{1,0:T(8,128)S(1)}, f32[72,128]{1,0:T(8,128)S(1)}, u32[]{:S(2)}, u32[]{:S(2)}) collective-permute-start(f32[72,128]{1,0:T(8,128)S(1)} %add_add_fusion.1), channel_id=1, source_target_pairs={{0,28},{8,20},{1,29},{9,21},{2,30},{10,22},{3,31},{11,23},{4,24},{... | collective-permute-start | bytes 110600 | tf_op jit(solution)/shard_map/ppermute | solution.py:263
  18.1 0.3 collective-permute-start.5
  18.4 0.6 %collective-permute-start.4 = (f32[72,128]{1,0:T(8,128)S(1)}, f32[72,128]{1,0:T(8,128)S(1)}, u32[]{:S(2)}, u32[]{:S(2)}) collective-permute-start(f32[72,128]{1,0:T(8,128)S(1)} %add_add_fusion.1), channel_id=1, source_target_pairs={{0,12},{8,4},{1,13},{9,5},{2,14},{10,6},{3,15},{11,7},{4,8},{12,0}... | collective-permute-start | bytes 110600 | tf_op jit(solution)/shard_map/ppermute | solution.py:263
  19.0 0.7 %collective-permute-done.6 = f32[72,128]{1,0:T(8,128)S(1)} collective-permute-done((f32[72,128]{1,0:T(8,128)S(1)}, f32[72,128]{1,0:T(8,128)S(1)}, u32[]{:S(2)}, u32[]{:S(2)}) %collective-permute-start.6) | collective-permute-done | bytes 36896 | tf_op jit(solution)/shard_map/ppermute | solution.py:263
  19.7 2.6 %collective-permute-done.5 = f32[72,128]{1,0:T(8,128)S(1)} collective-permute-done((f32[72,128]{1,0:T(8,128)S(1)}, f32[72,128]{1,0:T(8,128)S(1)}, u32[]{:S(2)}, u32[]{:S(2)}) %collective-permute-start.5) | collective-permute-done | bytes 36896 | tf_op jit(solution)/shard_map/ppermute | solution.py:263
  22.4 1.8 %collective-permute-start.7 = (f32[72,128]{1,0:T(8,128)S(1)}, f32[72,128]{1,0:T(8,128)S(1)}, u32[]{:S(2)}, u32[]{:S(2)}) collective-permute-start(f32[72,128]{1,0:T(8,128)S(1)} %add_add_fusion), channel_id=1, source_target_pairs={{0,40},{8,32},{1,41},{9,33},{2,42},{10,34},{3,43},{11,35},{4,44},{... | collective-permute-start | bytes 110600 | tf_op jit(solution)/shard_map/ppermute | solution.py:263
  24.2 1.6 %collective-permute-done.7 = f32[72,128]{1,0:T(8,128)S(1)} collective-permute-done((f32[72,128]{1,0:T(8,128)S(1)}, f32[72,128]{1,0:T(8,128)S(1)}, u32[]{:S(2)}, u32[]{:S(2)}) %collective-permute-start.7) | collective-permute-done | bytes 36896 | tf_op jit(solution)/shard_map/ppermute | solution.py:263
  25.9 4.4 %collective-permute-start.8 = (f32[72,128]{1,0:T(8,128)S(1)}, f32[72,128]{1,0:T(8,128)S(1)}, u32[]{:S(2)}, u32[]{:S(2)}) collective-permute-start(f32[72,128]{1,0:T(8,128)S(1)} %add.37), channel_id=1, source_target_pairs={{0,104},{8,96},{1,105},{9,97},{2,106},{10,98},{3,107},{11,99},{4,1... | collective-permute-start | bytes 110600 | tf_op jit(solution)/shard_map/ppermute | solution.py:263
  30.3 1.0 %preparation.1 = (f32[3,128,512]{2,1,0:T(8,128)S(1)}, bf16[128,128]{1,0:T(8,128)(2,1)S(1)}, bf16[128,512]{1,0:T(8,128)(2,1)S(1)}, f32[18,8,128]{2,1,0:T(8,128)S(1)}) custom-call(f32[3,6]{1,0:T(4,128)} %refs_0_.1, f32[3]{0:T(128)} %refs_1_.1, f32[128,512]{1,0:T(8,128)S(1)} %copy-done), custom_call_target="tpu_custom_call" | custom-call | tf_op jit(solution)/shard_map/preparation/pallas_call | solution.py:246
  31.4 0.6 %collective-permute-done.8 = f32[72,128]{1,0:T(8,128)S(1)} collective-permute-done((f32[72,128]{1,0:T(8,128)S(1)}, f32[72,128]{1,0:T(8,128)S(1)}, u32[]{:S(2)}, u32[]{:S(2)}) %collective-permute-start.8) | collective-permute-done | bytes 36896 | tf_op jit(solution)/shard_map/ppermute | solution.py:263
  32.0 4.8 %collective-permute-start.9 = (f32[72,128]{1,0:T(8,128)S(1)}, f32[72,128]{1,0:T(8,128)S(1)}, u32[]{:S(2)}, u32[]{:S(2)}) collective-permute-start(f32[72,128]{1,0:T(8,128)S(1)} %add.38), channel_id=1, source_target_pairs={{0,232},{8,224},{1,233},{9,225},{2,234},{10,226},{3,235},{11,227},... | collective-permute-start | bytes 110600 | tf_op jit(solution)/shard_map/ppermute | solution.py:263
  36.8 1.6 %collective-permute-done.9 = f32[72,128]{1,0:T(8,128)S(1)} collective-permute-done((f32[72,128]{1,0:T(8,128)S(1)}, f32[72,128]{1,0:T(8,128)S(1)}, u32[]{:S(2)}, u32[]{:S(2)}) %collective-permute-start.9) | collective-permute-done | bytes 36896 | tf_op jit(solution)/shard_map/ppermute | solution.py:263
  38.4 0.5 %collective-permute-start.10 = (f32[72,128]{1,0:T(8,128)S(1)}, f32[72,128]{1,0:T(8,128)S(1)}, u32[]{:S(2)}, u32[]{:S(2)}) collective-permute-start(f32[72,128]{1,0:T(8,128)S(1)} %add.39.refs_0_), channel_id=1, source_target_pairs={{0,8},{8,0},{1,9},{9,1},{2,10},{10,2},{3,11},{11,3},{4,12},{12,4},... | collective-permute-start | bytes 110600 | tf_op jit(solution)/shard_map/ppermute | solution.py:264
  38.9 0.9 %collective-permute-done.10.refs_1_ = f32[72,128]{1,0:T(8,128)S(1)} collective-permute-done((f32[72,128]{1,0:T(8,128)S(1)}, f32[72,128]{1,0:T(8,128)S(1)}, u32[]{:S(2)}, u32[]{:S(2)}) %collective-permute-start.10) | collective-permute-done | bytes 36896 | tf_op jit(solution)/shard_map/ppermute | solution.py:264
  39.8 2.1 %synthesis.1 = (bf16[18,128,512]{2,1,0:T(8,128)(2,1)}, f32[3,6]{1,0:T(4,128)}) custom-call(f32[72,128]{1,0:T(8,128)S(1)} %add.39.refs_0_, f32[72,128]{1,0:T(8,128)S(1)} %collective-permute-done.10.refs_1_, f32[3,128,512]{2,1,0:T(8,128)S(1)} %get-tuple-element.22.refs_2_, bf16[128,128]{1,0:T(8,128)(2,1)S(1)} %get-tuple-element.23.refs_3_, ...), custom_call_target="tpu_custom_call" | custom-call | tf_op jit(solution)/shard_map/synthesis/pallas_call | solution.py:266
  (9 shorter events, 0.1 us)
Async XLA Ops:
  0.6 29.7 %copy-start = (f32[128,512]{1,0:T(8,128)S(1)}, f32[128,512]{1,0:T(8,128)}, u32[]{:S(2)}) copy-start(f32[128,512]{1,0:T(8,128)} %refs_2_.1) | copy-start | bytes 786436
  4.4 4.2 %collective-permute-start = (f32[72,128]{1,0:T(8,128)S(1)}, f32[72,128]{1,0:T(8,128)S(1)}, u32[]{:S(2)}, u32[]{:S(2)}) collective-permute-start(f32[72,128]{1,0:T(8,128)S(1)} %get-tuple-element.16), channel_id=1, source_target_pairs={{0,8},{8,0},{1,9},{9,1},{2,10},{10,2},{3,11},{11,3},{4,12},{12,4},... | collective-permute-start | bytes 110600 | tf_op jit(solution)/shard_map/ppermute | solution.py:259
  8.6 4.6 %collective-permute-start.3 = (f32[72,128]{1,0:T(8,128)S(1)}, f32[72,128]{1,0:T(8,128)S(1)}, u32[]{:S(2)}, u32[]{:S(2)}) collective-permute-start(f32[72,128]{1,0:T(8,128)S(1)} %add.30), channel_id=1, source_target_pairs={{0,11},{8,3},{1,10},{9,2},{2,9},{10,1},{3,8},{11,0},{4,15},{12,7},... | collective-permute-start | bytes 110600 | tf_op jit(solution)/shard_map/ppermute | solution.py:263
  9.6 4.3 %collective-permute-start.2 = (f32[72,128]{1,0:T(8,128)S(1)}, f32[72,128]{1,0:T(8,128)S(1)}, u32[]{:S(2)}, u32[]{:S(2)}) collective-permute-start(f32[72,128]{1,0:T(8,128)S(1)} %add.30), channel_id=1, source_target_pairs={{0,2},{8,10},{1,3},{9,11},{2,0},{10,8},{3,1},{11,9},{4,6},{12,14},... | collective-permute-start | bytes 110600 | tf_op jit(solution)/shard_map/ppermute | solution.py:263
  10.1 4.8 %collective-permute-start.1 = (f32[72,128]{1,0:T(8,128)S(1)}, f32[72,128]{1,0:T(8,128)S(1)}, u32[]{:S(2)}, u32[]{:S(2)}) collective-permute-start(f32[72,128]{1,0:T(8,128)S(1)} %add.30), channel_id=1, source_target_pairs={{0,9},{8,1},{1,8},{9,0},{2,11},{10,3},{3,10},{11,2},{4,13},{12,5},... | collective-permute-start | bytes 110600 | tf_op jit(solution)/shard_map/ppermute | solution.py:263
  14.9 4.8 %collective-permute-start.6 = (f32[72,128]{1,0:T(8,128)S(1)}, f32[72,128]{1,0:T(8,128)S(1)}, u32[]{:S(2)}, u32[]{:S(2)}) collective-permute-start(f32[72,128]{1,0:T(8,128)S(1)} %add_add_fusion.1), channel_id=1, source_target_pairs={{0,28},{8,20},{1,29},{9,21},{2,30},{10,22},{3,31},{11,23},{4,24},{... | collective-permute-start | bytes 110600 | tf_op jit(solution)/shard_map/ppermute | solution.py:263
  18.1 4.3 %collective-permute-start.5 = (f32[72,128]{1,0:T(8,128)S(1)}, f32[72,128]{1,0:T(8,128)S(1)}, u32[]{:S(2)}, u32[]{:S(2)}) collective-permute-start(f32[72,128]{1,0:T(8,128)S(1)} %add_add_fusion.1), channel_id=1, source_target_pairs={{0,16},{8,24},{1,17},{9,25},{2,18},{10,26},{3,19},{11,27},{4,20},{... | collective-permute-start | bytes 110600 | tf_op jit(solution)/shard_map/ppermute | solution.py:263
  18.4 4.0 %collective-permute-start.4 = (f32[72,128]{1,0:T(8,128)S(1)}, f32[72,128]{1,0:T(8,128)S(1)}, u32[]{:S(2)}, u32[]{:S(2)}) collective-permute-start(f32[72,128]{1,0:T(8,128)S(1)} %add_add_fusion.1), channel_id=1, source_target_pairs={{0,12},{8,4},{1,13},{9,5},{2,14},{10,6},{3,15},{11,7},{4,8},{12,0}... | collective-permute-start | bytes 110600 | tf_op jit(solution)/shard_map/ppermute | solution.py:263
  22.4 3.5 %collective-permute-start.7 = (f32[72,128]{1,0:T(8,128)S(1)}, f32[72,128]{1,0:T(8,128)S(1)}, u32[]{:S(2)}, u32[]{:S(2)}) collective-permute-start(f32[72,128]{1,0:T(8,128)S(1)} %add_add_fusion), channel_id=1, source_target_pairs={{0,40},{8,32},{1,41},{9,33},{2,42},{10,34},{3,43},{11,35},{4,44},{... | collective-permute-start | bytes 110600 | tf_op jit(solution)/shard_map/ppermute | solution.py:263
  25.9 6.1 %collective-permute-start.8 = (f32[72,128]{1,0:T(8,128)S(1)}, f32[72,128]{1,0:T(8,128)S(1)}, u32[]{:S(2)}, u32[]{:S(2)}) collective-permute-start(f32[72,128]{1,0:T(8,128)S(1)} %add.37), channel_id=1, source_target_pairs={{0,104},{8,96},{1,105},{9,97},{2,106},{10,98},{3,107},{11,99},{4,1... | collective-permute-start | bytes 110600 | tf_op jit(solution)/shard_map/ppermute | solution.py:263
  32.0 6.4 %collective-permute-start.9 = (f32[72,128]{1,0:T(8,128)S(1)}, f32[72,128]{1,0:T(8,128)S(1)}, u32[]{:S(2)}, u32[]{:S(2)}) collective-permute-start(f32[72,128]{1,0:T(8,128)S(1)} %add.38), channel_id=1, source_target_pairs={{0,232},{8,224},{1,233},{9,225},{2,234},{10,226},{3,235},{11,227},... | collective-permute-start | bytes 110600 | tf_op jit(solution)/shard_map/ppermute | solution.py:263
  38.4 1.3 %collective-permute-start.10 = (f32[72,128]{1,0:T(8,128)S(1)}, f32[72,128]{1,0:T(8,128)S(1)}, u32[]{:S(2)}, u32[]{:S(2)}) collective-permute-start(f32[72,128]{1,0:T(8,128)S(1)} %add.39.refs_0_), channel_id=1, source_target_pairs={{0,8},{8,0},{1,9},{9,1},{2,10},{10,2},{3,11},{11,3},{4,12},{12,4},... | collective-permute-start | bytes 110600 | tf_op jit(solution)/shard_map/ppermute | solution.py:264

commit v4 on v3

--- a/solution.py
+++ b/solution.py
@@ -24,6 +24,12 @@
 
 CHIP = partners(lambda x, y, z, c: (x, y, z, 1 - c))
 EXCHANGES = (
+    (
+        partners(lambda x, y, z, c: (x, y, z ^ 2, 1 - c)),
+        partners(lambda x, y, z, c: (x, y, z ^ 1, c)),
+        partners(lambda x, y, z, c: (x, y, z ^ 3, 1 - c)),
+    ),
+    (partners(lambda x, y, z, c: (x, y, z ^ 7, 1 - c)),),
     (
         partners(lambda x, y, z, c: (x ^ 1, y, z, 1 - c)),
         partners(lambda x, y, z, c: (x ^ 2, y, z, c)),
@@ -34,15 +40,12 @@
         partners(lambda x, y, z, c: (x, y ^ 2, z, c)),
         partners(lambda x, y, z, c: (x, y ^ 3, z, 1 - c)),
     ),
-    (partners(lambda x, y, z, c: (x, y, z ^ 1, 1 - c)),),
-    (partners(lambda x, y, z, c: (x, y, z ^ 3, 1 - c)),),
-    (partners(lambda x, y, z, c: (x, y, z ^ 7, 1 - c)),),
 )
 
 
 def half_held():
     gx, gy = lax.axis_index("gx"), lax.axis_index("gy")
-    return (gx // 4 + gx + gy // 4 + gy) & 1
+    return (gx // 8 + gx + gy // 4 + gy) & 1
 
 
 def cosines(index, wave, total):
@@ -258,7 +261,7 @@
 
     held = mine + lax.ppermute(other, BOTH, CHIP)
     for at, exchange in enumerate(EXCHANGES):
-        if at == len(EXCHANGES) - 1:
+        if at == 2:
             held, prepared = lax.optimization_barrier((held, prepared))
         held = total([held] + [lax.ppermute(held, BOTH, pairs) for pairs in exchange])
     other = lax.ppermute(held, BOTH, CHIP)

time: 42 us -> 40.6 us (0.967)
  starting transfers between devices: 22.8 us -> 20.6 us
  waiting for transfers between devices: 11.5 us -> 12.1 us
    ppermute x9 -> x10, starting transfers between devices: 19 us -> 17.1 us  [per_device(): lax.ppermute(held, BOTH, pairs)]
    ppermute x9 -> x10, waiting for transfers between devices: 9.75 us -> 10.2 us  [per_device(): lax.ppermute(held, BOTH, pairs)]
  transfers between devices with their start and end apart: 11 -> 12, of which waited for: 10 -> 11; matrix products, arithmetic and copies ran while one was open for 0% -> 0% of each run, Pallas kernels for 2% -> 3%
where the time goes in v4:
time: 40.6 us; the launch traced here: 40.3 us
  starting transfers between devices  20.6 us (51%)
  waiting for transfers between devices  12.1 us (30%)
  Pallas kernels  6.89 us (17%)
  between operations  0.68 us (2%)
    ppermute x10, starting transfers between devices, per_device(): lax.ppermute(held, BOTH, pairs)  17.1 us
    ppermute x10, waiting for transfers between devices, per_device(): lax.ppermute(held, BOTH, pairs)  10.2 us
    pallas_call x1, Pallas kernels, per_device(): pl.pallas_call(lambda *refs: analysis(count, nx, ny, *refs), name='analys...  3.76 us
    ppermute x1, starting transfers between devices, per_device(): held = mine + lax.ppermute(other, BOTH, CHIP)  3.29 us
    pallas_call x1, Pallas kernels, per_device(): pl.pallas_call(lambda *refs: synthesis(levels, variables, *refs), name='s...  2.12 us
    ppermute x1, waiting for transfers between devices, per_device(): other = lax.ppermute(held, BOTH, CHIP)  1.06 us
    pallas_call x1, Pallas kernels, per_device(): pl.pallas_call(lambda *refs: preparation(levels, variables, nx, ny, *refs...  1.02 us
    ppermute x1, waiting for transfers between devices, per_device(): held = mine + lax.ppermute(other, BOTH, CHIP)  0.87 us
  transfers between devices with their start and end apart: 12, of which 11 were waited for; matrix products, arithmetic and copies ran while one was open for 0% of the time, Pallas kernels for 3%

profile of v4, /device:TPU:1, one launch (start us, length us, event | category | flops | bytes accessed | tf_op | source)
XLA Modules:
  0.0 40.3 jit_solution(16393208939834815433)
XLA Ops:
  0.6 3.8 %analysis.1 = (f32[72,128]{1,0:T(8,128)S(1)}, f32[72,128]{1,0:T(8,128)S(1)}) custom-call(f32[18,128,512]{2,1,0:T(8,128)} %bitcast.3, bf16[18,128,512]{2,1,0:T(8,128)(2,1)} %bitcast.4), custom_call_target="tpu_custom_call" | custom-call | tf_op jit(solution)/shard_map/analysis/pallas_call | solution.py:233
  4.4 3.3 %collective-permute-start = (f32[72,128]{1,0:T(8,128)S(1)}, f32[72,128]{1,0:T(8,128)S(1)}, u32[]{:S(2)}, u32[]{:S(2)}) collective-permute-start(f32[72,128]{1,0:T(8,128)S(1)} %get-tuple-element.16), channel_id=1, source_target_pairs={{0,8},{8,0},{1,9},{9,1},{2,10},{10,2},{3,11},{11,3},{4,12},{12,4},... | collective-permute-start | bytes 110600 | tf_op jit(solution)/shard_map/ppermute | solution.py:262
  7.7 0.9 %collective-permute-done = f32[72,128]{1,0:T(8,128)S(1)} collective-permute-done((f32[72,128]{1,0:T(8,128)S(1)}, f32[72,128]{1,0:T(8,128)S(1)}, u32[]{:S(2)}, u32[]{:S(2)}) %collective-permute-start) | collective-permute-done | bytes 36896 | tf_op jit(solution)/shard_map/ppermute | solution.py:262
  8.6 2.9 %collective-permute-start.3 = (f32[72,128]{1,0:T(8,128)S(1)}, f32[72,128]{1,0:T(8,128)S(1)}, u32[]{:S(2)}, u32[]{:S(2)}) collective-permute-start(f32[72,128]{1,0:T(8,128)S(1)} %add.33), channel_id=1, source_target_pairs={{0,104},{8,96},{1,105},{9,97},{2,106},{10,98},{3,107},{11,99},{4,1... | collective-permute-start | bytes 110600 | tf_op jit(solution)/shard_map/ppermute | solution.py:266
  11.4 1.2 %collective-permute-start.1 = (f32[72,128]{1,0:T(8,128)S(1)}, f32[72,128]{1,0:T(8,128)S(1)}, u32[]{:S(2)}, u32[]{:S(2)}) collective-permute-start(f32[72,128]{1,0:T(8,128)S(1)} %add.33), channel_id=1, source_target_pairs={{0,72},{8,64},{1,73},{9,65},{2,74},{10,66},{3,75},{11,67},{4,76},{... | collective-permute-start | bytes 110600 | tf_op jit(solution)/shard_map/ppermute | solution.py:266
  12.7 1.5 %collective-permute-done.3 = f32[72,128]{1,0:T(8,128)S(1)} collective-permute-done((f32[72,128]{1,0:T(8,128)S(1)}, f32[72,128]{1,0:T(8,128)S(1)}, u32[]{:S(2)}, u32[]{:S(2)}) %collective-permute-start.3) | collective-permute-done | bytes 36896 | tf_op jit(solution)/shard_map/ppermute | solution.py:266
  14.1 0.2 collective-permute-done.2
  14.4 1.3 %collective-permute-done.1 = f32[72,128]{1,0:T(8,128)S(1)} collective-permute-done((f32[72,128]{1,0:T(8,128)S(1)}, f32[72,128]{1,0:T(8,128)S(1)}, u32[]{:S(2)}, u32[]{:S(2)}) %collective-permute-start.1) | collective-permute-done | bytes 36896 | tf_op jit(solution)/shard_map/ppermute | solution.py:266
  15.7 4.0 %collective-permute-start.4 = (f32[72,128]{1,0:T(8,128)S(1)}, f32[72,128]{1,0:T(8,128)S(1)}, u32[]{:S(2)}, u32[]{:S(2)}) collective-permute-start(f32[72,128]{1,0:T(8,128)S(1)} %add_add_fusion.2), channel_id=1, source_target_pairs={{0,232},{8,224},{1,233},{9,225},{2,234},{10,226},{3,235},{11,227},... | collective-permute-start | bytes 110600 | tf_op jit(solution)/shard_map/ppermute | solution.py:266
  19.8 1.0 %preparation.1 = (f32[3,128,512]{2,1,0:T(8,128)S(1)}, bf16[128,128]{1,0:T(8,128)(2,1)S(1)}, bf16[128,512]{1,0:T(8,128)(2,1)S(1)}, f32[18,8,128]{2,1,0:T(8,128)S(1)}) custom-call(f32[3,6]{1,0:T(4,128)} %refs_0_.1, f32[3]{0:T(128)} %refs_1_.1, f32[128,512]{1,0:T(8,128)S(1)} %copy-done), custom_call_target="tpu_custom_call" | custom-call | tf_op jit(solution)/shard_map/preparation/pallas_call | solution.py:249
  20.8 0.6 %collective-permute-done.4 = f32[72,128]{1,0:T(8,128)S(1)} collective-permute-done((f32[72,128]{1,0:T(8,128)S(1)}, f32[72,128]{1,0:T(8,128)S(1)}, u32[]{:S(2)}, u32[]{:S(2)}) %collective-permute-start.4) | collective-permute-done | bytes 36896 | tf_op jit(solution)/shard_map/ppermute | solution.py:266
  21.4 2.4 %collective-permute-start.7 = (f32[72,128]{1,0:T(8,128)S(1)}, f32[72,128]{1,0:T(8,128)S(1)}, u32[]{:S(2)}, u32[]{:S(2)}) collective-permute-start(f32[72,128]{1,0:T(8,128)S(1)} %add.37), channel_id=1, source_target_pairs={{0,11},{8,3},{1,10},{9,2},{2,9},{10,1},{3,8},{11,0},{4,15},{12,7},... | collective-permute-start | bytes 110600 | tf_op jit(solution)/shard_map/ppermute | solution.py:266
  23.8 0.5 %collective-permute-start.6 = (f32[72,128]{1,0:T(8,128)S(1)}, f32[72,128]{1,0:T(8,128)S(1)}, u32[]{:S(2)}, u32[]{:S(2)}) collective-permute-start(f32[72,128]{1,0:T(8,128)S(1)} %add.37), channel_id=1, source_target_pairs={{0,2},{8,10},{1,3},{9,11},{2,0},{10,8},{3,1},{11,9},{4,6},{12,14},... | collective-permute-start | bytes 110600 | tf_op jit(solution)/shard_map/ppermute | solution.py:266
  24.3 0.9 %collective-permute-start.5 = (f32[72,128]{1,0:T(8,128)S(1)}, f32[72,128]{1,0:T(8,128)S(1)}, u32[]{:S(2)}, u32[]{:S(2)}) collective-permute-start(f32[72,128]{1,0:T(8,128)S(1)} %add.37), channel_id=1, source_target_pairs={{0,9},{8,1},{1,8},{9,0},{2,11},{10,3},{3,10},{11,2},{4,13},{12,5},... | collective-permute-start | bytes 110600 | tf_op jit(solution)/shard_map/ppermute | solution.py:266
  25.2 0.8 %collective-permute-done.7 = f32[72,128]{1,0:T(8,128)S(1)} collective-permute-done((f32[72,128]{1,0:T(8,128)S(1)}, f32[72,128]{1,0:T(8,128)S(1)}, u32[]{:S(2)}, u32[]{:S(2)}) %collective-permute-start.7) | collective-permute-done | bytes 36896 | tf_op jit(solution)/shard_map/ppermute | solution.py:266
  26.0 2.1 %collective-permute-done.6 = f32[72,128]{1,0:T(8,128)S(1)} collective-permute-done((f32[72,128]{1,0:T(8,128)S(1)}, f32[72,128]{1,0:T(8,128)S(1)}, u32[]{:S(2)}, u32[]{:S(2)}) %collective-permute-start.6) | collective-permute-done | bytes 36896 | tf_op jit(solution)/shard_map/ppermute | solution.py:266
  28.4 4.2 %collective-permute-start.10 = (f32[72,128]{1,0:T(8,128)S(1)}, f32[72,128]{1,0:T(8,128)S(1)}, u32[]{:S(2)}, u32[]{:S(2)}) collective-permute-start(f32[72,128]{1,0:T(8,128)S(1)} %add_add_fusion.1), channel_id=1, source_target_pairs={{0,28},{8,20},{1,29},{9,21},{2,30},{10,22},{3,31},{11,23},{4,24},{... | collective-permute-start | bytes 110600 | tf_op jit(solution)/shard_map/ppermute | solution.py:266
  32.6 0.3 collective-permute-start.9
  32.9 0.6 %collective-permute-start.8 = (f32[72,128]{1,0:T(8,128)S(1)}, f32[72,128]{1,0:T(8,128)S(1)}, u32[]{:S(2)}, u32[]{:S(2)}) collective-permute-start(f32[72,128]{1,0:T(8,128)S(1)} %add_add_fusion.1), channel_id=1, source_target_pairs={{0,12},{8,4},{1,13},{9,5},{2,14},{10,6},{3,15},{11,7},{4,8},{12,0}... | collective-permute-start | bytes 110600 | tf_op jit(solution)/shard_map/ppermute | solution.py:266
  33.6 0.7 %collective-permute-done.10 = f32[72,128]{1,0:T(8,128)S(1)} collective-permute-done((f32[72,128]{1,0:T(8,128)S(1)}, f32[72,128]{1,0:T(8,128)S(1)}, u32[]{:S(2)}, u32[]{:S(2)}) %collective-permute-start.10) | collective-permute-done | bytes 36896 | tf_op jit(solution)/shard_map/ppermute | solution.py:266
  34.3 2.6 %collective-permute-done.9 = f32[72,128]{1,0:T(8,128)S(1)} collective-permute-done((f32[72,128]{1,0:T(8,128)S(1)}, f32[72,128]{1,0:T(8,128)S(1)}, u32[]{:S(2)}, u32[]{:S(2)}) %collective-permute-start.9) | collective-permute-done | bytes 36896 | tf_op jit(solution)/shard_map/ppermute | solution.py:266
  36.9 0.2 collective-permute-start.11
  37.2 1.1 %collective-permute-done.11.refs_1_ = f32[72,128]{1,0:T(8,128)S(1)} collective-permute-done((f32[72,128]{1,0:T(8,128)S(1)}, f32[72,128]{1,0:T(8,128)S(1)}, u32[]{:S(2)}, u32[]{:S(2)}) %collective-permute-start.11) | collective-permute-done | bytes 36896 | tf_op jit(solution)/shard_map/ppermute | solution.py:267
  38.2 2.1 %synthesis.1 = (bf16[18,128,512]{2,1,0:T(8,128)(2,1)}, f32[3,6]{1,0:T(4,128)}) custom-call(f32[72,128]{1,0:T(8,128)S(1)} %add_add_fusion.refs_0_, f32[72,128]{1,0:T(8,128)S(1)} %collective-permute-done.11.refs_1_, f32[3,128,512]{2,1,0:T(8,128)S(1)} %get-tuple-element.22.refs_2_, bf16[128,128]{1,0:T(8,128)(2,1)S(1)} %get-tuple-element.23.refs_3_, ...), custom_call_target="tpu_custom_call" | custom-call | tf_op jit(solution)/shard_map/synthesis/pallas_call | solution.py:269
  (10 shorter events, 0.3 us)
Async XLA Ops:
  0.6 19.1 %copy-start = (f32[128,512]{1,0:T(8,128)S(1)}, f32[128,512]{1,0:T(8,128)}, u32[]{:S(2)}) copy-start(f32[128,512]{1,0:T(8,128)} %refs_2_.1) | copy-start | bytes 786436
  4.4 4.2 %collective-permute-start = (f32[72,128]{1,0:T(8,128)S(1)}, f32[72,128]{1,0:T(8,128)S(1)}, u32[]{:S(2)}, u32[]{:S(2)}) collective-permute-start(f32[72,128]{1,0:T(8,128)S(1)} %get-tuple-element.16), channel_id=1, source_target_pairs={{0,8},{8,0},{1,9},{9,1},{2,10},{10,2},{3,11},{11,3},{4,12},{12,4},... | collective-permute-start | bytes 110600 | tf_op jit(solution)/shard_map/ppermute | solution.py:262
  8.6 5.6 %collective-permute-start.3 = (f32[72,128]{1,0:T(8,128)S(1)}, f32[72,128]{1,0:T(8,128)S(1)}, u32[]{:S(2)}, u32[]{:S(2)}) collective-permute-start(f32[72,128]{1,0:T(8,128)S(1)} %add.33), channel_id=1, source_target_pairs={{0,104},{8,96},{1,105},{9,97},{2,106},{10,98},{3,107},{11,99},{4,1... | collective-permute-start | bytes 110600 | tf_op jit(solution)/shard_map/ppermute | solution.py:266
  11.4 3.0 %collective-permute-start.2 = (f32[72,128]{1,0:T(8,128)S(1)}, f32[72,128]{1,0:T(8,128)S(1)}, u32[]{:S(2)}, u32[]{:S(2)}) collective-permute-start(f32[72,128]{1,0:T(8,128)S(1)} %add.33), channel_id=1, source_target_pairs={{0,32},{8,40},{1,33},{9,41},{2,34},{10,42},{3,35},{11,43},{4,36},{... | collective-permute-start | bytes 110600 | tf_op jit(solution)/shard_map/ppermute | solution.py:266
  11.4 4.3 %collective-permute-start.1 = (f32[72,128]{1,0:T(8,128)S(1)}, f32[72,128]{1,0:T(8,128)S(1)}, u32[]{:S(2)}, u32[]{:S(2)}) collective-permute-start(f32[72,128]{1,0:T(8,128)S(1)} %add.33), channel_id=1, source_target_pairs={{0,72},{8,64},{1,73},{9,65},{2,74},{10,66},{3,75},{11,67},{4,76},{... | collective-permute-start | bytes 110600 | tf_op jit(solution)/shard_map/ppermute | solution.py:266
  15.7 5.7 %collective-permute-start.4 = (f32[72,128]{1,0:T(8,128)S(1)}, f32[72,128]{1,0:T(8,128)S(1)}, u32[]{:S(2)}, u32[]{:S(2)}) collective-permute-start(f32[72,128]{1,0:T(8,128)S(1)} %add_add_fusion.2), channel_id=1, source_target_pairs={{0,232},{8,224},{1,233},{9,225},{2,234},{10,226},{3,235},{11,227},... | collective-permute-start | bytes 110600 | tf_op jit(solution)/shard_map/ppermute | solution.py:266
  21.4 4.6 %collective-permute-start.7 = (f32[72,128]{1,0:T(8,128)S(1)}, f32[72,128]{1,0:T(8,128)S(1)}, u32[]{:S(2)}, u32[]{:S(2)}) collective-permute-start(f32[72,128]{1,0:T(8,128)S(1)} %add.37), channel_id=1, source_target_pairs={{0,11},{8,3},{1,10},{9,2},{2,9},{10,1},{3,8},{11,0},{4,15},{12,7},... | collective-permute-start | bytes 110600 | tf_op jit(solution)/shard_map/ppermute | solution.py:266
  23.8 4.3 %collective-permute-start.6 = (f32[72,128]{1,0:T(8,128)S(1)}, f32[72,128]{1,0:T(8,128)S(1)}, u32[]{:S(2)}, u32[]{:S(2)}) collective-permute-start(f32[72,128]{1,0:T(8,128)S(1)} %add.37), channel_id=1, source_target_pairs={{0,2},{8,10},{1,3},{9,11},{2,0},{10,8},{3,1},{11,9},{4,6},{12,14},... | collective-permute-start | bytes 110600 | tf_op jit(solution)/shard_map/ppermute | solution.py:266
  24.3 4.0 %collective-permute-start.5 = (f32[72,128]{1,0:T(8,128)S(1)}, f32[72,128]{1,0:T(8,128)S(1)}, u32[]{:S(2)}, u32[]{:S(2)}) collective-permute-start(f32[72,128]{1,0:T(8,128)S(1)} %add.37), channel_id=1, source_target_pairs={{0,9},{8,1},{1,8},{9,0},{2,11},{10,3},{3,10},{11,2},{4,13},{12,5},... | collective-permute-start | bytes 110600 | tf_op jit(solution)/shard_map/ppermute | solution.py:266
  28.4 5.9 %collective-permute-start.10 = (f32[72,128]{1,0:T(8,128)S(1)}, f32[72,128]{1,0:T(8,128)S(1)}, u32[]{:S(2)}, u32[]{:S(2)}) collective-permute-start(f32[72,128]{1,0:T(8,128)S(1)} %add_add_fusion.1), channel_id=1, source_target_pairs={{0,28},{8,20},{1,29},{9,21},{2,30},{10,22},{3,31},{11,23},{4,24},{... | collective-permute-start | bytes 110600 | tf_op jit(solution)/shard_map/ppermute | solution.py:266
  32.6 4.3 %collective-permute-start.9 = (f32[72,128]{1,0:T(8,128)S(1)}, f32[72,128]{1,0:T(8,128)S(1)}, u32[]{:S(2)}, u32[]{:S(2)}) collective-permute-start(f32[72,128]{1,0:T(8,128)S(1)} %add_add_fusion.1), channel_id=1, source_target_pairs={{0,16},{8,24},{1,17},{9,25},{2,18},{10,26},{3,19},{11,27},{4,20},{... | collective-permute-start | bytes 110600 | tf_op jit(solution)/shard_map/ppermute | solution.py:266
  32.9 4.0 %collective-permute-start.8 = (f32[72,128]{1,0:T(8,128)S(1)}, f32[72,128]{1,0:T(8,128)S(1)}, u32[]{:S(2)}, u32[]{:S(2)}) collective-permute-start(f32[72,128]{1,0:T(8,128)S(1)} %add_add_fusion.1), channel_id=1, source_target_pairs={{0,12},{8,4},{1,13},{9,5},{2,14},{10,6},{3,15},{11,7},{4,8},{12,0}... | collective-permute-start | bytes 110600 | tf_op jit(solution)/shard_map/ppermute | solution.py:266
  36.9 1.3 %collective-permute-start.11 = (f32[72,128]{1,0:T(8,128)S(1)}, f32[72,128]{1,0:T(8,128)S(1)}, u32[]{:S(2)}, u32[]{:S(2)}) collective-permute-start(f32[72,128]{1,0:T(8,128)S(1)} %add_add_fusion.refs_0_), channel_id=1, source_target_pairs={{0,8},{8,0},{1,9},{9,1},{2,10},{10,2},{3,11},{11,3},{4,12},{12,4},... | collective-permute-start | bytes 110600 | tf_op jit(solution)/shard_map/ppermute | solution.py:267

commit v5 on v4

--- a/solution.py
+++ b/solution.py
@@ -74,23 +74,49 @@
     return jnp.dot(a, b, preferred_element_type=F32)
 
 
-CHUNK = 6
-
-
-def analysis(
-    count, nx, ny, p_hbm, f_hbm, mine_ref, other_ref, p_buf, f_buf, p_sem, f_sem, w_ref, out_ref
+CHUNKS = (5, 4)
+
+
+def transformed(p_buf, f_buf, start, size, row_table, w, out_ref):
+    wide = 4 * MODES
+    lane_group = iota((8, wide), 1) // MODES
+    parts = []
+    for k in range(start, start + size):
+        diff = jnp.concatenate(split(f_buf[k].astype(F32) - p_buf[k]), axis=0)
+        both = dot(row_table, diff)
+        parts.append(both[:MODES] + both[MODES:])
+    part = jnp.concatenate(split(jnp.concatenate(parts, axis=0)), axis=0)
+    both = dot(part, w)
+    both = both[: size * MODES] + both[size * MODES :]
+    both = both[:, :wide] + both[:, wide:]
+    for i in range(size):
+        coefs = both[MODES * i : MODES * (i + 1)]
+        tile = coefs[:8]
+        for q in range(1, 4):
+            tile = jnp.where(lane_group == q, coefs[8 * q : 8 * q + 8], tile)
+        out_ref[8 * (start + i) : 8 * (start + i) + 8, :] = tile
+
+
+def analysis_other(
+    count, nx, ny, p_hbm, f_hbm, other_ref, p_mine, f_mine, w_ref, r_ref, p_buf, f_buf, p_sem, f_sem
 ):
     rows, cols = p_hbm.shape[1:]
+    half = count // 2
+    mine = half_held() * half
     copies = []
-    for at, start in enumerate(range(0, count, CHUNK)):
-        chunk = pl.ds(start, CHUNK)
-        pair = (
-            pltpu.make_async_copy(p_hbm.at[chunk], p_buf.at[chunk], p_sem.at[at]),
-            pltpu.make_async_copy(f_hbm.at[chunk], f_buf.at[chunk], f_sem.at[at]),
-        )
+    for at, size in enumerate(CHUNKS):
+        there, here = pl.ds(half - mine + sum(CHUNKS[:at]), size), pl.ds(sum(CHUNKS[:at]), size)
+        copies.append((
+            pltpu.make_async_copy(p_hbm.at[there], p_buf.at[here], p_sem.at[at]),
+            pltpu.make_async_copy(f_hbm.at[there], f_buf.at[here], f_sem.at[at]),
+        ))
+    copies.append((
+        pltpu.make_async_copy(p_hbm.at[pl.ds(mine, half)], p_mine, p_sem.at[len(CHUNKS)]),
+        pltpu.make_async_copy(f_hbm.at[pl.ds(mine, half)], f_mine, f_sem.at[len(CHUNKS)]),
+    ))
+    for pair in copies:
         for copy in pair:
             copy.start()
-        copies.append(pair)
 
     row0 = lax.axis_index("gx") * rows
     col0 = lax.axis_index("gy") * cols
@@ -104,32 +130,17 @@
     row_table = jnp.concatenate(
         [jnp.concatenate([high, high], axis=1), jnp.concatenate([low, low], axis=1)], axis=0
     )
-    lane_group = iota((8, wide), 1) // MODES
-
-    for pair, start in zip(copies, range(0, count, CHUNK)):
-        for copy in pair:
+    r_ref[...] = row_table
+    for at, size in enumerate(CHUNKS):
+        for copy in copies[at]:
             copy.wait()
-        parts = []
-        for k in range(start, start + CHUNK):
-            diff = jnp.concatenate(split(f_buf[k].astype(F32) - p_buf[k]), axis=0)
-            both = dot(row_table, diff)
-            parts.append(both[:MODES] + both[MODES:])
-        part = jnp.concatenate(split(jnp.concatenate(parts, axis=0)), axis=0)
-        both = dot(part, w_ref[...])
-        both = both[: CHUNK * MODES] + both[CHUNK * MODES :]
-        both = both[:, :wide] + both[:, wide:]
-        for i in range(CHUNK):
-            coefs = both[MODES * i : MODES * (i + 1)]
-            tile = coefs[:8]
-            for q in range(1, 4):
-                tile = jnp.where(lane_group == q, coefs[8 * q : 8 * q + 8], tile)
-            line = 8 * (start + i)
-            out_ref[line : line + 8, :] = tile
-    half = out_ref.shape[0] // 2
-    first, second = out_ref[:half, :], out_ref[half:, :]
-    held = half_held() == 0
-    mine_ref[...] = jnp.where(held, first, second)
-    other_ref[...] = jnp.where(held, second, first)
+        transformed(p_buf, f_buf, sum(CHUNKS[:at]), size, row_table, w_ref[...], other_ref)
+    for copy in copies[-1]:
+        copy.wait()
+
+
+def analysis_mine(count, p_ref, f_ref, w_ref, r_ref, mine_ref):
+    transformed(p_ref, f_ref, 0, count // 2, r_ref[...], w_ref[...], mine_ref)
 
 
 def preparation(
@@ -210,6 +221,10 @@
         copy.wait()
 
 
+def in_hbm(value):
+    return pltpu.with_memory_space_constraint(value, pltpu.HBM)
+
+
 def in_vmem(value):
     return pltpu.with_memory_space_constraint(value, pltpu.VMEM)
 
@@ -230,21 +245,39 @@
     vmem = pl.BlockSpec(memory_space=pltpu.VMEM)
     smem = pl.BlockSpec(memory_space=pltpu.SMEM)
 
-    mine, other = pl.pallas_call(
-        lambda *refs: analysis(count, nx, ny, *refs),
-        name="analysis",
-        out_shape=(pltpu.VMEM((lines // 2, wide), F32), pltpu.VMEM((lines // 2, wide), F32)),
+    half = count // 2
+    other, *kept = pl.pallas_call(
+        lambda *refs: analysis_other(count, nx, ny, *refs),
+        name="analysis_other",
+        out_shape=(
+            pltpu.VMEM((lines // 2, wide), F32),
+            pltpu.VMEM((half, rows, cols), F32),
+            pltpu.VMEM((half, rows, cols), BF16),
+            pltpu.VMEM((cols, 2 * wide), BF16),
+            pltpu.VMEM((2 * MODES, 2 * rows), BF16),
+        ),
         in_specs=[anywhere, anywhere],
-        out_specs=(vmem, vmem),
+        out_specs=(vmem,) * 5,
+        compiler_params=pltpu.CompilerParams(vmem_limit_bytes=24 << 20),
         scratch_shapes=[
-            pltpu.VMEM((count, rows, cols), F32),
-            pltpu.VMEM((count, rows, cols), BF16),
-            pltpu.SemaphoreType.DMA((count // CHUNK,)),
-            pltpu.SemaphoreType.DMA((count // CHUNK,)),
-            pltpu.VMEM((cols, 2 * wide), BF16),
-            pltpu.VMEM((lines, wide), F32),
+            pltpu.VMEM((half, rows, cols), F32),
+            pltpu.VMEM((half, rows, cols), BF16),
+            pltpu.SemaphoreType.DMA((len(CHUNKS) + 1,)),
+            pltpu.SemaphoreType.DMA((len(CHUNKS) + 1,)),
         ],
-    )(prognostic_values.reshape(count, rows, cols), forcing_host_values.reshape(count, rows, cols))
+    )(
+        in_hbm(prognostic_values.reshape(count, rows, cols)),
+        in_hbm(forcing_host_values.reshape(count, rows, cols)),
+    )
+    arriving = lax.ppermute(other, BOTH, CHIP)
+    mine = pl.pallas_call(
+        lambda *refs: analysis_mine(count, *refs),
+        name="analysis_mine",
+        out_shape=pltpu.VMEM((lines // 2, wide), F32),
+        in_specs=[vmem] * 4,
+        out_specs=vmem,
+        compiler_params=pltpu.CompilerParams(vmem_limit_bytes=24 << 20),
+    )(*map(in_vmem, kept))
 
     prepared = pl.pallas_call(
         lambda *refs: preparation(levels, variables, nx, ny, *refs),
@@ -259,11 +292,12 @@
         out_specs=(vmem, vmem, vmem, vmem),
     )(strength, level_height, in_vmem(pbl_height))
 
-    held = mine + lax.ppermute(other, BOTH, CHIP)
+    held = mine + arriving
     for at, exchange in enumerate(EXCHANGES):
         if at == 2:
             held, prepared = lax.optimization_barrier((held, prepared))
-        held = total([held] + [lax.ppermute(held, BOTH, pairs) for pairs in exchange])
+        arrived = [lax.ppermute(held, BOTH, pairs) for pairs in reversed(exchange)]
+        held = total([held] + arrived)
     other = lax.ppermute(held, BOTH, CHIP)
 
     tendency, energy = pl.pallas_call(

time: 40.6 us -> 41.8 us (1.030)
  starting transfers between devices: 20.6 us -> 22.7 us
  waiting for transfers between devices: 12.1 us -> 10.8 us
    ppermute x1, starting transfers between devices: 0.24 us -> 1.99 us  [per_device(): other = lax.ppermute(held, BOTH, CHIP)]
    ppermute x11, waiting for transfers between devices: 11 us -> 9.97 us  [the longest x10 9.97 us: per_device(): arrived = [lax.ppermute(held, BOTH, pairs) for pairs in reversed(exchange)]]
    pallas_call x1 -> x2, Pallas kernels: 3.76 us -> 3.99 us  [the longest x1 3.13 us: per_device(): pl.pallas_call(lambda *refs: analysis_other(count, nx, ny, *refs), name='...]
  transfers between devices with their start and end apart: 12 -> 12, of which waited for: 11 -> 10; matrix products, arithmetic and copies ran while one was open for 0% -> 0% of each run, Pallas kernels for 3% -> 5%
where the time goes in v5:
time: 41.8 us; the launch traced here: 41.4 us
  starting transfers between devices  22.7 us (54%)
  waiting for transfers between devices  10.8 us (26%)
  Pallas kernels  7.13 us (17%)
  between operations  0.7 us (2%)
    ppermute x10, starting transfers between devices, per_device(): arrived = [lax.ppermute(held, BOTH, pairs) for pairs in reversed(exchange)]  17.4 us
    ppermute x10, waiting for transfers between devices, per_device(): arrived = [lax.ppermute(held, BOTH, pairs) for pairs in reversed(exchange)]  9.97 us
    ppermute x1, starting transfers between devices, per_device(): arriving = lax.ppermute(other, BOTH, CHIP)  3.29 us
    pallas_call x1, Pallas kernels, per_device(): pl.pallas_call(lambda *refs: analysis_other(count, nx, ny, *refs), name='...  3.13 us
    pallas_call x1, Pallas kernels, per_device(): pl.pallas_call(lambda *refs: synthesis(levels, variables, *refs), name='s...  2.12 us
    ppermute x1, starting transfers between devices, per_device(): other = lax.ppermute(held, BOTH, CHIP)  1.99 us
    pallas_call x1, Pallas kernels, per_device(): pl.pallas_call(lambda *refs: preparation(levels, variables, nx, ny, *refs...  1.02 us
    ppermute x1, waiting for transfers between devices, per_device(): other = lax.ppermute(held, BOTH, CHIP)  0.87 us
  transfers between devices with their start and end apart: 12, of which 10 were waited for; matrix products, arithmetic and copies ran while one was open for 0% of the time, Pallas kernels for 5%

profile of v5, /device:TPU:1, one launch (start us, length us, event | category | flops | bytes accessed | tf_op | source)
XLA Modules:
  0.0 41.4 jit_solution(11810091101742522437)
XLA Ops:
  0.6 3.1 %analysis_other.1 = (f32[72,128]{1,0:T(8,128)S(1)}, f32[9,128,512]{2,1,0:T(8,128)S(1)}, bf16[9,128,512]{2,1,0:T(8,128)(2,1)S(1)}, bf16[512,256]{1,0:T(8,128)(2,1)S(1)}, bf16[64,256]{1,0:T(8,128)(2,1)S(1)}) custom-call(f32[18,128,512]{2,1,0:T(8,128)} %bitcast.3, bf16[18,128,512]{2,1,0:T(8,128)(2,1)} %bitcast.4), custom_call_target="tpu_custom_call" | custom-call | tf_op jit(solution)/shard_map/analysis_other/pallas_call | solution.py:249
  3.8 3.3 %collective-permute-start = (f32[72,128]{1,0:T(8,128)S(1)}, f32[72,128]{1,0:T(8,128)S(1)}, u32[]{:S(2)}, u32[]{:S(2)}) collective-permute-start(f32[72,128]{1,0:T(8,128)S(1)} %get-tuple-element.22), channel_id=1, source_target_pairs={{0,8},{8,0},{1,9},{9,1},{2,10},{10,2},{3,11},{11,3},{4,12},{12,4},... | collective-permute-start | bytes 110600 | tf_op jit(solution)/shard_map/ppermute | solution.py:272
  7.1 0.9 %analysis_mine.1 = f32[72,128]{1,0:T(8,128)S(1)} custom-call(f32[9,128,512]{2,1,0:T(8,128)S(1)} %get-tuple-element.18.refs_0_, bf16[9,128,512]{2,1,0:T(8,128)(2,1)S(1)} %get-tuple-element.19.refs_1_, bf16[512,256]{1,0:T(8,128)(2,1)S(1)} %get-tuple-element.20.refs_2_, bf16[64,256]{1,0:T(8,128)(2,1)S(1)} %get-tuple-element.21.refs_3_), custom_call_target="tpu_custom_call" | custom-call | tf_op jit(solution)/shard_map/analysis_mine/pallas_call | solution.py:273
  8.0 2.8 %collective-permute-start.1 = (f32[72,128]{1,0:T(8,128)S(1)}, f32[72,128]{1,0:T(8,128)S(1)}, u32[]{:S(2)}, u32[]{:S(2)}) collective-permute-start(f32[72,128]{1,0:T(8,128)S(1)} %add.33), channel_id=1, source_target_pairs={{0,104},{8,96},{1,105},{9,97},{2,106},{10,98},{3,107},{11,99},{4,1... | collective-permute-start | bytes 110600 | tf_op jit(solution)/shard_map/ppermute | solution.py:299
  10.8 1.3 %collective-permute-start.3 = (f32[72,128]{1,0:T(8,128)S(1)}, f32[72,128]{1,0:T(8,128)S(1)}, u32[]{:S(2)}, u32[]{:S(2)}) collective-permute-start(f32[72,128]{1,0:T(8,128)S(1)} %add.33), channel_id=1, source_target_pairs={{0,72},{8,64},{1,73},{9,65},{2,74},{10,66},{3,75},{11,67},{4,76},{... | collective-permute-start | bytes 110600 | tf_op jit(solution)/shard_map/ppermute | solution.py:299
  12.2 1.5 %collective-permute-done.1 = f32[72,128]{1,0:T(8,128)S(1)} collective-permute-done((f32[72,128]{1,0:T(8,128)S(1)}, f32[72,128]{1,0:T(8,128)S(1)}, u32[]{:S(2)}, u32[]{:S(2)}) %collective-permute-start.1) | collective-permute-done | bytes 36896 | tf_op jit(solution)/shard_map/ppermute | solution.py:299
  13.8 1.3 %collective-permute-done.3 = f32[72,128]{1,0:T(8,128)S(1)} collective-permute-done((f32[72,128]{1,0:T(8,128)S(1)}, f32[72,128]{1,0:T(8,128)S(1)}, u32[]{:S(2)}, u32[]{:S(2)}) %collective-permute-start.3) | collective-permute-done | bytes 36896 | tf_op jit(solution)/shard_map/ppermute | solution.py:299
  15.1 4.0 %collective-permute-start.4 = (f32[72,128]{1,0:T(8,128)S(1)}, f32[72,128]{1,0:T(8,128)S(1)}, u32[]{:S(2)}, u32[]{:S(2)}) collective-permute-start(f32[72,128]{1,0:T(8,128)S(1)} %add_add_fusion.2), channel_id=1, source_target_pairs={{0,232},{8,224},{1,233},{9,225},{2,234},{10,226},{3,235},{11,227},... | collective-permute-start | bytes 110600 | tf_op jit(solution)/shard_map/ppermute | solution.py:299
  19.1 1.0 %preparation.1 = (f32[3,128,512]{2,1,0:T(8,128)S(1)}, bf16[128,128]{1,0:T(8,128)(2,1)S(1)}, bf16[128,512]{1,0:T(8,128)(2,1)S(1)}, f32[18,8,128]{2,1,0:T(8,128)S(1)}) custom-call(f32[3,6]{1,0:T(4,128)} %refs_0_.1, f32[3]{0:T(128)} %refs_1_.1, f32[128,512]{1,0:T(8,128)S(1)} %copy-done), custom_call_target="tpu_custom_call" | custom-call | tf_op jit(solution)/shard_map/preparation/pallas_call | solution.py:282
  20.2 0.6 %collective-permute-done.4 = f32[72,128]{1,0:T(8,128)S(1)} collective-permute-done((f32[72,128]{1,0:T(8,128)S(1)}, f32[72,128]{1,0:T(8,128)S(1)}, u32[]{:S(2)}, u32[]{:S(2)}) %collective-permute-start.4) | collective-permute-done | bytes 36896 | tf_op jit(solution)/shard_map/ppermute | solution.py:299
  20.8 2.4 %collective-permute-start.5 = (f32[72,128]{1,0:T(8,128)S(1)}, f32[72,128]{1,0:T(8,128)S(1)}, u32[]{:S(2)}, u32[]{:S(2)}) collective-permute-start(f32[72,128]{1,0:T(8,128)S(1)} %add.37), channel_id=1, source_target_pairs={{0,11},{8,3},{1,10},{9,2},{2,9},{10,1},{3,8},{11,0},{4,15},{12,7},... | collective-permute-start | bytes 110600 | tf_op jit(solution)/shard_map/ppermute | solution.py:299
  23.2 0.5 %collective-permute-start.6 = (f32[72,128]{1,0:T(8,128)S(1)}, f32[72,128]{1,0:T(8,128)S(1)}, u32[]{:S(2)}, u32[]{:S(2)}) collective-permute-start(f32[72,128]{1,0:T(8,128)S(1)} %add.37), channel_id=1, source_target_pairs={{0,2},{8,10},{1,3},{9,11},{2,0},{10,8},{3,1},{11,9},{4,6},{12,14},... | collective-permute-start | bytes 110600 | tf_op jit(solution)/shard_map/ppermute | solution.py:299
  23.7 0.9 %collective-permute-start.7 = (f32[72,128]{1,0:T(8,128)S(1)}, f32[72,128]{1,0:T(8,128)S(1)}, u32[]{:S(2)}, u32[]{:S(2)}) collective-permute-start(f32[72,128]{1,0:T(8,128)S(1)} %add.37), channel_id=1, source_target_pairs={{0,9},{8,1},{1,8},{9,0},{2,11},{10,3},{3,10},{11,2},{4,13},{12,5},... | collective-permute-start | bytes 110600 | tf_op jit(solution)/shard_map/ppermute | solution.py:299
  24.6 0.8 %collective-permute-done.5 = f32[72,128]{1,0:T(8,128)S(1)} collective-permute-done((f32[72,128]{1,0:T(8,128)S(1)}, f32[72,128]{1,0:T(8,128)S(1)}, u32[]{:S(2)}, u32[]{:S(2)}) %collective-permute-start.5) | collective-permute-done | bytes 36896 | tf_op jit(solution)/shard_map/ppermute | solution.py:299
  25.4 2.1 %collective-permute-done.6 = f32[72,128]{1,0:T(8,128)S(1)} collective-permute-done((f32[72,128]{1,0:T(8,128)S(1)}, f32[72,128]{1,0:T(8,128)S(1)}, u32[]{:S(2)}, u32[]{:S(2)}) %collective-permute-start.6) | collective-permute-done | bytes 36896 | tf_op jit(solution)/shard_map/ppermute | solution.py:299
  27.5 0.2 collective-permute-done.7
  27.8 2.8 %collective-permute-start.10 = (f32[72,128]{1,0:T(8,128)S(1)}, f32[72,128]{1,0:T(8,128)S(1)}, u32[]{:S(2)}, u32[]{:S(2)}) collective-permute-start(f32[72,128]{1,0:T(8,128)S(1)} %add_add_fusion.1), channel_id=1, source_target_pairs={{0,12},{8,4},{1,13},{9,5},{2,14},{10,6},{3,15},{11,7},{4,8},{12,0}... | collective-permute-start | bytes 110600 | tf_op jit(solution)/shard_map/ppermute | solution.py:299
  30.5 1.5 %collective-permute-start.8 = (f32[72,128]{1,0:T(8,128)S(1)}, f32[72,128]{1,0:T(8,128)S(1)}, u32[]{:S(2)}, u32[]{:S(2)}) collective-permute-start(f32[72,128]{1,0:T(8,128)S(1)} %add_add_fusion.1), channel_id=1, source_target_pairs={{0,28},{8,20},{1,29},{9,21},{2,30},{10,22},{3,31},{11,23},{4,24},{... | collective-permute-start | bytes 110600 | tf_op jit(solution)/shard_map/ppermute | solution.py:299
  32.1 1.1 %collective-permute-start.9 = (f32[72,128]{1,0:T(8,128)S(1)}, f32[72,128]{1,0:T(8,128)S(1)}, u32[]{:S(2)}, u32[]{:S(2)}) collective-permute-start(f32[72,128]{1,0:T(8,128)S(1)} %add_add_fusion.1), channel_id=1, source_target_pairs={{0,16},{8,24},{1,17},{9,25},{2,18},{10,26},{3,19},{11,27},{4,20},{... | collective-permute-start | bytes 110600 | tf_op jit(solution)/shard_map/ppermute | solution.py:299
  33.2 2.0 %collective-permute-done.8 = f32[72,128]{1,0:T(8,128)S(1)} collective-permute-done((f32[72,128]{1,0:T(8,128)S(1)}, f32[72,128]{1,0:T(8,128)S(1)}, u32[]{:S(2)}, u32[]{:S(2)}) %collective-permute-start.8) | collective-permute-done | bytes 36896 | tf_op jit(solution)/shard_map/ppermute | solution.py:299
  35.1 1.3 %collective-permute-done.9 = f32[72,128]{1,0:T(8,128)S(1)} collective-permute-done((f32[72,128]{1,0:T(8,128)S(1)}, f32[72,128]{1,0:T(8,128)S(1)}, u32[]{:S(2)}, u32[]{:S(2)}) %collective-permute-start.9) | collective-permute-done | bytes 36896 | tf_op jit(solution)/shard_map/ppermute | solution.py:299
  36.4 2.0 %collective-permute-start.11 = (f32[72,128]{1,0:T(8,128)S(1)}, f32[72,128]{1,0:T(8,128)S(1)}, u32[]{:S(2)}, u32[]{:S(2)}) collective-permute-start(f32[72,128]{1,0:T(8,128)S(1)} %add_add_fusion.refs_0_), channel_id=1, source_target_pairs={{0,8},{8,0},{1,9},{9,1},{2,10},{10,2},{3,11},{11,3},{4,12},{12,4},... | collective-permute-start | bytes 110600 | tf_op jit(solution)/shard_map/ppermute | solution.py:301
  38.4 0.9 %collective-permute-done.11.refs_1_ = f32[72,128]{1,0:T(8,128)S(1)} collective-permute-done((f32[72,128]{1,0:T(8,128)S(1)}, f32[72,128]{1,0:T(8,128)S(1)}, u32[]{:S(2)}, u32[]{:S(2)}) %collective-permute-start.11) | collective-permute-done | bytes 36896 | tf_op jit(solution)/shard_map/ppermute | solution.py:301
  39.3 2.1 %synthesis.1 = (bf16[18,128,512]{2,1,0:T(8,128)(2,1)}, f32[3,6]{1,0:T(4,128)}) custom-call(f32[72,128]{1,0:T(8,128)S(1)} %add_add_fusion.refs_0_, f32[72,128]{1,0:T(8,128)S(1)} %collective-permute-done.11.refs_1_, f32[3,128,512]{2,1,0:T(8,128)S(1)} %get-tuple-element.28.refs_2_, bf16[128,128]{1,0:T(8,128)(2,1)S(1)} %get-tuple-element.29.refs_3_, ...), custom_call_target="tpu_custom_call" | custom-call | tf_op jit(solution)/shard_map/synthesis/pallas_call | solution.py:303
  (11 shorter events, 0.2 us)
Async XLA Ops:
  3.8 15.4 %copy-start = (f32[128,512]{1,0:T(8,128)S(1)}, f32[128,512]{1,0:T(8,128)}, u32[]{:S(2)}) copy-start(f32[128,512]{1,0:T(8,128)} %refs_2_.1) | copy-start | bytes 786436
  3.8 4.2 %collective-permute-start = (f32[72,128]{1,0:T(8,128)S(1)}, f32[72,128]{1,0:T(8,128)S(1)}, u32[]{:S(2)}, u32[]{:S(2)}) collective-permute-start(f32[72,128]{1,0:T(8,128)S(1)} %get-tuple-element.22), channel_id=1, source_target_pairs={{0,8},{8,0},{1,9},{9,1},{2,10},{10,2},{3,11},{11,3},{4,12},{12,4},... | collective-permute-start | bytes 110600 | tf_op jit(solution)/shard_map/ppermute | solution.py:272
  8.0 5.7 %collective-permute-start.1 = (f32[72,128]{1,0:T(8,128)S(1)}, f32[72,128]{1,0:T(8,128)S(1)}, u32[]{:S(2)}, u32[]{:S(2)}) collective-permute-start(f32[72,128]{1,0:T(8,128)S(1)} %add.33), channel_id=1, source_target_pairs={{0,104},{8,96},{1,105},{9,97},{2,106},{10,98},{3,107},{11,99},{4,1... | collective-permute-start | bytes 110600 | tf_op jit(solution)/shard_map/ppermute | solution.py:299
  10.8 3.0 %collective-permute-start.2 = (f32[72,128]{1,0:T(8,128)S(1)}, f32[72,128]{1,0:T(8,128)S(1)}, u32[]{:S(2)}, u32[]{:S(2)}) collective-permute-start(f32[72,128]{1,0:T(8,128)S(1)} %add.33), channel_id=1, source_target_pairs={{0,32},{8,40},{1,33},{9,41},{2,34},{10,42},{3,35},{11,43},{4,36},{... | collective-permute-start | bytes 110600 | tf_op jit(solution)/shard_map/ppermute | solution.py:299
  10.8 4.3 %collective-permute-start.3 = (f32[72,128]{1,0:T(8,128)S(1)}, f32[72,128]{1,0:T(8,128)S(1)}, u32[]{:S(2)}, u32[]{:S(2)}) collective-permute-start(f32[72,128]{1,0:T(8,128)S(1)} %add.33), channel_id=1, source_target_pairs={{0,72},{8,64},{1,73},{9,65},{2,74},{10,66},{3,75},{11,67},{4,76},{... | collective-permute-start | bytes 110600 | tf_op jit(solution)/shard_map/ppermute | solution.py:299
  15.1 5.6 %collective-permute-start.4 = (f32[72,128]{1,0:T(8,128)S(1)}, f32[72,128]{1,0:T(8,128)S(1)}, u32[]{:S(2)}, u32[]{:S(2)}) collective-permute-start(f32[72,128]{1,0:T(8,128)S(1)} %add_add_fusion.2), channel_id=1, source_target_pairs={{0,232},{8,224},{1,233},{9,225},{2,234},{10,226},{3,235},{11,227},... | collective-permute-start | bytes 110600 | tf_op jit(solution)/shard_map/ppermute | solution.py:299
  20.8 4.6 %collective-permute-start.5 = (f32[72,128]{1,0:T(8,128)S(1)}, f32[72,128]{1,0:T(8,128)S(1)}, u32[]{:S(2)}, u32[]{:S(2)}) collective-permute-start(f32[72,128]{1,0:T(8,128)S(1)} %add.37), channel_id=1, source_target_pairs={{0,11},{8,3},{1,10},{9,2},{2,9},{10,1},{3,8},{11,0},{4,15},{12,7},... | collective-permute-start | bytes 110600 | tf_op jit(solution)/shard_map/ppermute | solution.py:299
  23.2 4.3 %collective-permute-start.6 = (f32[72,128]{1,0:T(8,128)S(1)}, f32[72,128]{1,0:T(8,128)S(1)}, u32[]{:S(2)}, u32[]{:S(2)}) collective-permute-start(f32[72,128]{1,0:T(8,128)S(1)} %add.37), channel_id=1, source_target_pairs={{0,2},{8,10},{1,3},{9,11},{2,0},{10,8},{3,1},{11,9},{4,6},{12,14},... | collective-permute-start | bytes 110600 | tf_op jit(solution)/shard_map/ppermute | solution.py:299
  23.7 4.0 %collective-permute-start.7 = (f32[72,128]{1,0:T(8,128)S(1)}, f32[72,128]{1,0:T(8,128)S(1)}, u32[]{:S(2)}, u32[]{:S(2)}) collective-permute-start(f32[72,128]{1,0:T(8,128)S(1)} %add.37), channel_id=1, source_target_pairs={{0,9},{8,1},{1,8},{9,0},{2,11},{10,3},{3,10},{11,2},{4,13},{12,5},... | collective-permute-start | bytes 110600 | tf_op jit(solution)/shard_map/ppermute | solution.py:299
  27.8 5.4 %collective-permute-start.10 = (f32[72,128]{1,0:T(8,128)S(1)}, f32[72,128]{1,0:T(8,128)S(1)}, u32[]{:S(2)}, u32[]{:S(2)}) collective-permute-start(f32[72,128]{1,0:T(8,128)S(1)} %add_add_fusion.1), channel_id=1, source_target_pairs={{0,12},{8,4},{1,13},{9,5},{2,14},{10,6},{3,15},{11,7},{4,8},{12,0}... | collective-permute-start | bytes 110600 | tf_op jit(solution)/shard_map/ppermute | solution.py:299
  30.5 4.6 %collective-permute-start.8 = (f32[72,128]{1,0:T(8,128)S(1)}, f32[72,128]{1,0:T(8,128)S(1)}, u32[]{:S(2)}, u32[]{:S(2)}) collective-permute-start(f32[72,128]{1,0:T(8,128)S(1)} %add_add_fusion.1), channel_id=1, source_target_pairs={{0,28},{8,20},{1,29},{9,21},{2,30},{10,22},{3,31},{11,23},{4,24},{... | collective-permute-start | bytes 110600 | tf_op jit(solution)/shard_map/ppermute | solution.py:299
  32.1 4.3 %collective-permute-start.9 = (f32[72,128]{1,0:T(8,128)S(1)}, f32[72,128]{1,0:T(8,128)S(1)}, u32[]{:S(2)}, u32[]{:S(2)}) collective-permute-start(f32[72,128]{1,0:T(8,128)S(1)} %add_add_fusion.1), channel_id=1, source_target_pairs={{0,16},{8,24},{1,17},{9,25},{2,18},{10,26},{3,19},{11,27},{4,20},{... | collective-permute-start | bytes 110600 | tf_op jit(solution)/shard_map/ppermute | solution.py:299
  36.4 2.9 %collective-permute-start.11 = (f32[72,128]{1,0:T(8,128)S(1)}, f32[72,128]{1,0:T(8,128)S(1)}, u32[]{:S(2)}, u32[]{:S(2)}) collective-permute-start(f32[72,128]{1,0:T(8,128)S(1)} %add_add_fusion.refs_0_), channel_id=1, source_target_pairs={{0,8},{8,0},{1,9},{9,1},{2,10},{10,2},{3,11},{11,3},{4,12},{12,4},... | collective-permute-start | bytes 110600 | tf_op jit(solution)/shard_map/ppermute | solution.py:301
